TPU v7x, 32 devices: a whole 2x2x4 slice. The times are simulated.
32 devices in a mesh: lat: 4 (over y, x), lon: 4 (over z), ens: 2 (over core).
Axes of the slice: x: 2, y: 2, z: 4, core: 2. Of those that a mesh axis runs over, the one named last changes fastest.
Arguments:
- parameters: float32 [2, 128, 32, 512], P(None, 'ens', 'lat', 'lon'), may hold values from -1.2 to 1.2, as said below
- initial_height: float32 [32, 512], P('lat', 'lon'), may hold values from -6 to 6
- initial_speed: float32 [2, 32, 512], P(None, 'lat', 'lon'), may hold values from -4 to 4
- obs_slots: int32 [2, 16, 16, 8], P(None, ('lat', 'lon')), may hold values from -1 to 1023, as said below
- obs_values: float32 [2, 16, 16, 8], P(None, ('lat', 'lon')), may hold values from -6 to 6
- obs_precision: float32 [2, 16, 16, 8], P(None, ('lat', 'lon')), may hold values from 0 to 2, as said below
Outputs:
- calibrated: float32 [2, 128, 32, 512], P(None, 'ens', 'lat', 'lon')
Inputs may be any that keep to these rules, and one draw needn't show every extreme that they name: `obs_slots`: for each iteration and owner, the live slots towards one receiver come first and name distinct cells of the owner's block (local index row * 128 + column); no cell is named twice by one owner in one iteration; in each iteration some receiving block has all 8 slots live from every owner. `obs_precision`: zero exactly where the matching slot of obs_slots (with receiver and owner swapped) is empty, 0.5 or more elsewhere. `parameters`: friction rates lie in 0.02 to 0.2, forcing in -1.2 to 1.2.
All inputs are finite; a program needn't handle non-finite values.
Results may differ from a plain program's by a relative error of at most 0.0003.
Values sent between devices are 32-bit elements; how exact they have to be, the bound alone decides.
A program may use at most 64 MiB of HBM per device.

v0:
```python
import math

import jax
import jax.numpy as jnp
from jax import lax
from jax.sharding import PartitionSpec as P

STEPS = 6
ITERS = 2


depth_step = 0.7
gravity_step = 0.7
coriolis = 0.1


def padded_2(value, sides, width, wrap):
    for axis, dim in sides:
        peers, length = (lax.axis_size(axis), value.shape[dim])
        up = [(i, (i + 1) % peers) for i in range(peers if wrap else peers - 1)]
        down = [(j, i) for i, j in up]
        last = lax.slice_in_dim(value, length - width, length, axis=dim)
        leading = lax.slice_in_dim(value, 0, width, axis=dim)
        before = lax.ppermute(last, axis, up)
        after = lax.ppermute(leading, axis, down)
        value = jnp.concatenate([before, value, after], axis=dim)
    return value


def wall_rows(padded):
    row_count = padded.shape[-2]
    position = lax.axis_index("lat")
    last_block = lax.axis_size("lat") - 1
    row_ids = lax.broadcasted_iota(jnp.int32, (row_count, 1), 0)
    lower_wall = jnp.logical_and(row_ids == 0, position == 0)
    upper_wall = jnp.logical_and(row_ids == row_count - 1, position == last_block)
    keep_rows = jnp.logical_not(jnp.logical_or(lower_wall, upper_wall))
    return padded * keep_rows.astype(padded.dtype)


def advance(height, speeds, friction, forcing):
    east_padded = padded_2(speeds[0], (("lon", 2),), 1, True)
    north_padded = padded_2(speeds[1], (("lat", 1),), 1, False)
    east_diff = east_padded[:, :, 2:] - east_padded[:, :, :-2]
    north_diff = north_padded[:, 2:, :] - north_padded[:, :-2, :]
    height = height - depth_step * (east_diff + north_diff) + forcing
    padded_height = padded_2(height, (("lat", 1), ("lon", 2)), 1, True)
    padded_height = wall_rows(padded_height)
    slope_east = padded_height[:, 1:-1, 2:] - padded_height[:, 1:-1, :-2]
    slope_north = padded_height[:, 2:, 1:-1] - padded_height[:, :-2, 1:-1]
    eastward = (1.0 - friction) * speeds[0] - gravity_step * slope_east + coriolis * speeds[1]
    northward = (1.0 - friction) * speeds[1] - gravity_step * slope_north - coriolis * speeds[0]
    return (height, jnp.stack([eastward, northward]))


def forward(parameters, initial_height, initial_speed):
    members = parameters.shape[1]
    height = jnp.broadcast_to(initial_height, (members,) + initial_height.shape)
    speeds = jnp.broadcast_to(initial_speed[:, None], (2, members) + initial_height.shape)
    for substep in range(STEPS):
        height, speeds = advance(height, speeds, parameters[0], parameters[1])
    return height


def predict(height, cells):
    flattened = height.reshape(height.shape[0], -1)
    wanted = cells.reshape(-1)
    picked = jnp.take(flattened, jnp.clip(wanted, 0, flattened.shape[1] - 1), axis=1)
    picked = jnp.where(wanted[None, :] >= 0, picked, jnp.float32(0.0))
    return picked.T.reshape(cells.shape[0], -1)


def gram_terms(predicted, observed, precision):
    members = predicted.shape[1]
    centre = jnp.mean(predicted, axis=1, keepdims=True)
    spread = predicted - centre
    weighted = spread * precision[:, None]
    misfit = observed[:, None] - predicted
    gram_part = jnp.dot(spread.T, weighted, precision=lax.Precision.HIGHEST) / members
    cross_part = jnp.dot(weighted.T, misfit, precision=lax.Precision.HIGHEST) / math.sqrt(members)
    return (gram_part, cross_part)


def solve_weights(gram_part, cross_part):
    members = gram_part.shape[0]
    system = jnp.eye(members, dtype=jnp.float32) + gram_part
    factor = jnp.linalg.cholesky(system)
    weights = jax.scipy.linalg.cho_solve((factor, True), cross_part) / math.sqrt(members)
    return weights - jnp.mean(weights, axis=0, keepdims=True)


def per_device(parameters, initial_height, initial_speed, obs_slots, obs_values, obs_precision):
    owners = obs_slots.shape[2]
    slot_count = obs_slots.shape[3]
    members_here = parameters.shape[1]
    member_block = lax.axis_index("ens")
    owner_values, owner_precision = (
        lax.all_to_all(obs_values[:, 0], ("lat", "lon"), split_axis=1, concat_axis=1, tiled=True),
        lax.all_to_all(
            obs_precision[:, 0], ("lat", "lon"), split_axis=1, concat_axis=1, tiled=True
        ),
    )
    for iteration in range(ITERS):
        height = forward(parameters, initial_height, initial_speed)
        outgoing = predict(height, obs_slots[iteration, 0])
        received = outgoing
        observed = owner_values[iteration]
        precision = owner_precision[iteration]
        received = received.reshape(owners, slot_count, members_here)
        gathered = lax.all_gather(received, "ens", axis=2, tiled=True)
        members = gathered.shape[2]
        gram_part, cross_part = gram_terms(
            gathered.reshape(-1, members), observed.reshape(-1), precision.reshape(-1)
        )
        gram_part, cross_part = lax.psum((gram_part, cross_part), ("lat", "lon"))
        centred = solve_weights(gram_part, cross_part)
        local_weights = lax.dynamic_slice_in_dim(
            centred, member_block * members_here, members_here, 1
        )
        starting = jnp.zeros(
            (2, members_here, parameters.shape[2] * parameters.shape[3]), jnp.float32
        )
        pieces = lax.all_gather(parameters, "ens", axis=1, tiled=True)
        stacked = pieces.reshape(pieces.shape[0], pieces.shape[1], -1)
        increment = starting + jnp.einsum(
            "pjc,jm->pmc", stacked, local_weights, precision=lax.Precision.HIGHEST
        )
        parameters = parameters + increment.reshape(parameters.shape)
    return parameters


def solution(mesh):
    placed = (
        P(None, "ens", "lat", "lon"),
        P("lat", "lon"),
        P(None, "lat", "lon"),
        P(None, ("lat", "lon"), None, None),
        P(None, ("lat", "lon"), None, None),
        P(None, ("lat", "lon"), None, None),
    )
    return jax.shard_map(
        per_device,
        mesh=mesh,
        in_specs=placed,
        out_specs=P(None, "ens", "lat", "lon"),
        check_vma=False,
    )
```

profile of v0, /device:TPU:0, one launch (start us, length us, event | category | flops | bytes accessed | tf_op | source)
XLA Modules:
  0.0 799.9 jit_solution(9738654765726643208)
XLA Ops:
  9.5 5.5 collective-permute-start.3
  15.3 4.2 collective-permute-start
  19.6 6.5 collective-permute-done
  26.2 4.8 collective-permute-done.1
  42.6 12.8 %collective-permute-done.6 = f32[64,10,1]{2,1,0:T(8,128)S(1)} collective-permute-done((f32[64,10,1]{2,1,0:T(8,128)S(1)}, f32[64,10,1]{2,1,0:T(8,128)S(1)}, u32[]{:S(2)}, u32[]{:S(2)}) %collective-permute-start.6) | collective-permute-done | bytes 2592 | tf_op jit(solution)/shard_map/ppermute | solution.py:24
  55.4 6.8 collective-permute-done.7
  64.6 4.5 collective-permute-start.11
  71.5 10.8 %collective-permute-done.8 = f32[64,8,1]{2,1,0:T(8,128)S(1)} collective-permute-done((f32[64,8,1]{2,1,0:T(8,128)S(1)}, f32[64,8,1]{2,1,0:T(8,128)S(1)}, u32[]{:S(2)}, u32[]{:S(2)}) %collective-permute-start.8) | collective-permute-done | bytes 2080 | tf_op jit(solution)/shard_map/ppermute | solution.py:25
  90.0 3.5 collective-permute-start.15
  93.5 12.5 %collective-permute-done.14 = f32[64,10,1]{2,1,0:T(8,128)S(1)} collective-permute-done((f32[64,10,1]{2,1,0:T(8,128)S(1)}, f32[64,10,1]{2,1,0:T(8,128)S(1)}, u32[]{:S(2)}, u32[]{:S(2)}) %collective-permute-start.14) | collective-permute-done | bytes 2592 | tf_op jit(solution)/shard_map/ppermute | solution.py:24
  106.0 5.6 collective-permute-done.15
  114.0 4.5 collective-permute-start.19
  118.7 3.0 collective-permute-start.16
  121.7 10.4 %collective-permute-done.16 = f32[64,8,1]{2,1,0:T(8,128)S(1)} collective-permute-done((f32[64,8,1]{2,1,0:T(8,128)S(1)}, f32[64,8,1]{2,1,0:T(8,128)S(1)}, u32[]{:S(2)}, u32[]{:S(2)}) %collective-permute-start.16) | collective-permute-done | bytes 2080 | tf_op jit(solution)/shard_map/ppermute | solution.py:25
  140.3 3.3 collective-permute-start.23
  144.3 4.1 all-to-all-start.1
  148.4 7.9 collective-permute-done.22
  156.3 5.7 collective-permute-done.23
  164.3 2.9 collective-permute-start.24
  168.5 4.5 collective-permute-start.27
  173.1 5.0 collective-permute-done.24
  184.9 3.2 collective-permute-start.31
  188.6 12.2 %collective-permute-done.30 = f32[64,10,1]{2,1,0:T(8,128)S(1)} collective-permute-done((f32[64,10,1]{2,1,0:T(8,128)S(1)}, f32[64,10,1]{2,1,0:T(8,128)S(1)}, u32[]{:S(2)}, u32[]{:S(2)}) %collective-permute-start.30) | collective-permute-done | bytes 2592 | tf_op jit(solution)/shard_map/ppermute | solution.py:24
  200.8 6.1 collective-permute-done.31
  211.7 4.5 collective-permute-start.35
  216.2 5.8 collective-permute-done.32
  230.1 3.3 collective-permute-start.39
  233.4 4.1 all-to-all-start
  239.0 7.4 collective-permute-done.38
  246.4 6.6 collective-permute-done.39
  259.3 5.2 collective-permute-start.43
  265.9 3.2 collective-permute-done.40
  278.0 104.7 %all-reduce.7.cloned.1.call-done = (f32[128,128]{1,0:T(8,128)}, f32[128,128]{0,1:T(8,128)}) async-done(((f32[128,128]{1,0:T(8,128)}, f32[128,128]{0,1:T(8,128)}), (f32[128,128]{1,0:T(8,128)}, f32[128,128]{0,1:T(8,128)})) %all-reduce.7.cloned.1.call-update) | async-done | bytes 131088 | tf_op jit(solution)/shard_map/psum | solution.py:115
  384.4 11.7 %cholesky.44 = f32[128,128]{1,0:T(8,128)S(1)} custom-call(f32[128,128]{1,0:T(8,128)S(1)} %fusion.151), custom_call_target="Cholesky" | custom-call | tf_op jit(solution)/shard_map/jit(cholesky)/cholesky | solution.py:87
  397.5 9.8 %custom-call.8 = f32[1,128,128]{1,2,0:T(8,128)S(1)} custom-call(f32[1,128,128]{2,1,0:T(8,128)S(1)} %fusion.135), custom_call_target="InvertDiagBlocksLowerTriangular" | custom-call | tf_op jit(solution)/shard_map/jit(_cho_solve)/triangular_solve | solution.py:88
  418.1 3.1 collective-permute-start.47
  421.1 12.8 %collective-permute-done.46 = f32[64,10,1]{2,1,0:T(8,128)S(1)} collective-permute-done((f32[64,10,1]{2,1,0:T(8,128)S(1)}, f32[64,10,1]{2,1,0:T(8,128)S(1)}, u32[]{:S(2)}, u32[]{:S(2)}) %collective-permute-start.46) | collective-permute-done | bytes 2592 | tf_op jit(solution)/shard_map/ppermute | solution.py:24
  433.9 5.6 collective-permute-done.47
  441.9 4.8 collective-permute-start.51
  449.0 10.4 %collective-permute-done.48 = f32[64,8,1]{2,1,0:T(8,128)S(1)} collective-permute-done((f32[64,8,1]{2,1,0:T(8,128)S(1)}, f32[64,8,1]{2,1,0:T(8,128)S(1)}, u32[]{:S(2)}, u32[]{:S(2)}) %collective-permute-start.48) | collective-permute-done | bytes 2080 | tf_op jit(solution)/shard_map/ppermute | solution.py:25
  460.0 2.7 collective-permute-start.52
  470.9 12.6 %collective-permute-done.54 = f32[64,10,1]{2,1,0:T(8,128)S(1)} collective-permute-done((f32[64,10,1]{2,1,0:T(8,128)S(1)}, f32[64,10,1]{2,1,0:T(8,128)S(1)}, u32[]{:S(2)}, u32[]{:S(2)}) %collective-permute-start.54) | collective-permute-done | bytes 2592 | tf_op jit(solution)/shard_map/ppermute | solution.py:24
  483.5 6.3 collective-permute-done.55
  492.3 4.5 collective-permute-start.59
  499.6 7.2 collective-permute-done.56
  506.8 3.5 collective-permute-done.57
  520.7 12.8 %collective-permute-done.62 = f32[64,10,1]{2,1,0:T(8,128)S(1)} collective-permute-done((f32[64,10,1]{2,1,0:T(8,128)S(1)}, f32[64,10,1]{2,1,0:T(8,128)S(1)}, u32[]{:S(2)}, u32[]{:S(2)}) %collective-permute-start.62) | collective-permute-done | bytes 2592 | tf_op jit(solution)/shard_map/ppermute | solution.py:24
  533.4 5.7 collective-permute-done.63
  541.6 4.5 collective-permute-start.67
  546.3 3.3 collective-permute-start.64
  549.6 7.2 collective-permute-done.64
  556.7 3.5 collective-permute-done.65
  570.7 12.8 %collective-permute-done.70 = f32[64,10,1]{2,1,0:T(8,128)S(1)} collective-permute-done((f32[64,10,1]{2,1,0:T(8,128)S(1)}, f32[64,10,1]{2,1,0:T(8,128)S(1)}, u32[]{:S(2)}, u32[]{:S(2)}) %collective-permute-start.70) | collective-permute-done | bytes 2592 | tf_op jit(solution)/shard_map/ppermute | solution.py:24
  583.4 4.5 collective-permute-done.71
  590.4 4.5 collective-permute-start.75
  597.8 7.3 collective-permute-done.72
  605.0 3.1 collective-permute-done.73
  618.4 11.9 %collective-permute-done.78 = f32[64,10,1]{2,1,0:T(8,128)S(1)} collective-permute-done((f32[64,10,1]{2,1,0:T(8,128)S(1)}, f32[64,10,1]{2,1,0:T(8,128)S(1)}, u32[]{:S(2)}, u32[]{:S(2)}) %collective-permute-start.78) | collective-permute-done | bytes 2592 | tf_op jit(solution)/shard_map/ppermute | solution.py:24
  630.3 4.9 collective-permute-done.79
  640.1 4.5 collective-permute-start.83
  646.2 3.6 collective-permute-done.81
  657.9 105.2 %all-reduce.5.cloned.1.call-done = (f32[128,128]{1,0:T(8,128)}, f32[128,128]{0,1:T(8,128)}) async-done(((f32[128,128]{1,0:T(8,128)}, f32[128,128]{0,1:T(8,128)}), (f32[128,128]{1,0:T(8,128)}, f32[128,128]{0,1:T(8,128)})) %all-reduce.5.cloned.1.call-update) | async-done | bytes 131088 | tf_op jit(solution)/shard_map/psum | solution.py:115
  764.7 11.7 %cholesky.55 = f32[128,128]{1,0:T(8,128)S(1)} custom-call(f32[128,128]{1,0:T(8,128)S(1)} %fusion.146), custom_call_target="Cholesky" | custom-call | tf_op jit(solution)/shard_map/jit(cholesky)/cholesky | solution.py:87
  777.8 9.8 %custom-call.9 = f32[1,128,128]{1,2,0:T(8,128)S(1)} custom-call(f32[1,128,128]{2,1,0:T(8,128)S(1)} %fusion.136), custom_call_target="InvertDiagBlocksLowerTriangular" | custom-call | tf_op jit(solution)/shard_map/jit(_cho_solve)/triangular_solve | solution.py:88
  (344 shorter events, 172.6 us)
Async XLA Ops:
  8.2 22.9 %collective-permute-start.2 = (f32[64,1,128]{2,1,0:T(1,128)S(1)}, f32[64,1,128]{2,1,0:T(1,128)S(1)}, u32[]{:S(2)}, u32[]{:S(2)}) collective-permute-start(f32[64,1,128]{2,1,0:T(1,128)S(1)} %broadcast_in_dim.82), channel_id=1, source_target_pairs={{8,0},{16,8},{24,16},{9,1},{17,9},{25,17},{10,2},{18,10},{26,18},{... | collective-permute-start | bytes 98312 | tf_op jit(solution)/shard_map/ppermute | solution.py:25
  9.5 21.5 %collective-permute-start.3 = (f32[64,1,128]{2,1,0:T(1,128)S(1)}, f32[64,1,128]{2,1,0:T(1,128)S(1)}, u32[]{:S(2)}, u32[]{:S(2)}) collective-permute-start(f32[64,1,128]{2,1,0:T(1,128)S(1)} %broadcast_in_dim.83), channel_id=1, source_target_pairs={{0,8},{8,16},{16,24},{1,9},{9,17},{17,25},{2,10},{10,18},{18,26},{... | collective-permute-start | bytes 98312 | tf_op jit(solution)/shard_map/ppermute | solution.py:24
  15.3 10.9 %collective-permute-start = (f32[64,8,1]{2,1,0:T(8,128)S(1)}, f32[64,8,1]{2,1,0:T(8,128)S(1)}, u32[]{:S(2)}, u32[]{:S(2)}) collective-permute-start(f32[64,8,1]{2,1,0:T(8,128)S(1)} %broadcast_in_dim.78), channel_id=1, source_target_pairs={{2,0},{4,2},{6,4},{0,6},{3,1},{5,3},{7,5},{1,7},{10,8},{12,10},{14... | collective-permute-start | bytes 6152 | tf_op jit(solution)/shard_map/ppermute | solution.py:25
  19.6 11.4 %collective-permute-start.1 = (f32[64,8,1]{2,1,0:T(8,128)S(1)}, f32[64,8,1]{2,1,0:T(8,128)S(1)}, u32[]{:S(2)}, u32[]{:S(2)}) collective-permute-start(f32[64,8,1]{2,1,0:T(8,128)S(1)} %broadcast_in_dim.79), channel_id=1, source_target_pairs={{0,2},{2,4},{4,6},{6,0},{1,3},{3,5},{5,7},{7,1},{8,10},{10,12},{12... | collective-permute-start | bytes 6152 | tf_op jit(solution)/shard_map/ppermute | solution.py:24
  38.7 16.6 %collective-permute-start.6 = (f32[64,10,1]{2,1,0:T(8,128)S(1)}, f32[64,10,1]{2,1,0:T(8,128)S(1)}, u32[]{:S(2)}, u32[]{:S(2)}) collective-permute-start(f32[64,10,1]{2,1,0:T(8,128)S(1)} %get-tuple-element.56), channel_id=1, source_target_pairs={{0,2},{2,4},{4,6},{6,0},{1,3},{3,5},{5,7},{7,1},{8,10},{10,12},{12... | collective-permute-start | bytes 7688 | tf_op jit(solution)/shard_map/ppermute | solution.py:24
  40.4 21.8 %collective-permute-start.7 = (f32[64,10,1]{2,1,0:T(8,128)S(1)}, f32[64,10,1]{2,1,0:T(8,128)S(1)}, u32[]{:S(2)}, u32[]{:S(2)}) collective-permute-start(f32[64,10,1]{2,1,0:T(8,128)S(1)} %get-tuple-element.57), channel_id=1, source_target_pairs={{2,0},{4,2},{6,4},{0,6},{3,1},{5,3},{7,5},{1,7},{10,8},{12,10},{14... | collective-permute-start | bytes 7688 | tf_op jit(solution)/shard_map/ppermute | solution.py:25
  63.3 18.9 %collective-permute-start.10 = (f32[64,1,128]{2,1,0:T(1,128)S(1)}, f32[64,1,128]{2,1,0:T(1,128)S(1)}, u32[]{:S(2)}, u32[]{:S(2)}) collective-permute-start(f32[64,1,128]{2,1,0:T(1,128)S(1)} %get-tuple-element.114), channel_id=1, source_target_pairs={{8,0},{16,8},{24,16},{9,1},{17,9},{25,17},{10,2},{18,10},{26,18},{... | collective-permute-start | bytes 98312 | tf_op jit(solution)/shard_map/ppermute | solution.py:25
  64.6 17.6 %collective-permute-start.11 = (f32[64,1,128]{2,1,0:T(1,128)S(1)}, f32[64,1,128]{2,1,0:T(1,128)S(1)}, u32[]{:S(2)}, u32[]{:S(2)}) collective-permute-start(f32[64,1,128]{2,1,0:T(1,128)S(1)} %get-tuple-element.115), channel_id=1, source_target_pairs={{0,8},{8,16},{16,24},{1,9},{9,17},{17,25},{2,10},{10,18},{18,26},{... | collective-permute-start | bytes 98312 | tf_op jit(solution)/shard_map/ppermute | solution.py:24
  69.3 12.9 %collective-permute-start.8 = (f32[64,8,1]{2,1,0:T(8,128)S(1)}, f32[64,8,1]{2,1,0:T(8,128)S(1)}, u32[]{:S(2)}, u32[]{:S(2)}) collective-permute-start(f32[64,8,1]{2,1,0:T(8,128)S(1)} %get-tuple-element.112), channel_id=1, source_target_pairs={{2,0},{4,2},{6,4},{0,6},{3,1},{5,3},{7,5},{1,7},{10,8},{12,10},{14... | collective-permute-start | bytes 6152 | tf_op jit(solution)/shard_map/ppermute | solution.py:25
  71.4 10.8 %collective-permute-start.9 = (f32[64,8,1]{2,1,0:T(8,128)S(1)}, f32[64,8,1]{2,1,0:T(8,128)S(1)}, u32[]{:S(2)}, u32[]{:S(2)}) collective-permute-start(f32[64,8,1]{2,1,0:T(8,128)S(1)} %get-tuple-element.113), channel_id=1, source_target_pairs={{0,2},{2,4},{4,6},{6,0},{1,3},{3,5},{5,7},{7,1},{8,10},{10,12},{12... | collective-permute-start | bytes 6152 | tf_op jit(solution)/shard_map/ppermute | solution.py:24
  89.7 16.4 %collective-permute-start.14 = (f32[64,10,1]{2,1,0:T(8,128)S(1)}, f32[64,10,1]{2,1,0:T(8,128)S(1)}, u32[]{:S(2)}, u32[]{:S(2)}) collective-permute-start(f32[64,10,1]{2,1,0:T(8,128)S(1)} %get-tuple-element.54), channel_id=1, source_target_pairs={{0,2},{2,4},{4,6},{6,0},{1,3},{3,5},{5,7},{7,1},{8,10},{10,12},{12... | collective-permute-start | bytes 7688 | tf_op jit(solution)/shard_map/ppermute | solution.py:24
  90.0 21.6 %collective-permute-start.15 = (f32[64,10,1]{2,1,0:T(8,128)S(1)}, f32[64,10,1]{2,1,0:T(8,128)S(1)}, u32[]{:S(2)}, u32[]{:S(2)}) collective-permute-start(f32[64,10,1]{2,1,0:T(8,128)S(1)} %get-tuple-element.55), channel_id=1, source_target_pairs={{2,0},{4,2},{6,4},{0,6},{3,1},{5,3},{7,5},{1,7},{10,8},{12,10},{14... | collective-permute-start | bytes 7688 | tf_op jit(solution)/shard_map/ppermute | solution.py:25
  112.7 19.3 %collective-permute-start.18 = (f32[64,1,128]{2,1,0:T(1,128)S(1)}, f32[64,1,128]{2,1,0:T(1,128)S(1)}, u32[]{:S(2)}, u32[]{:S(2)}) collective-permute-start(f32[64,1,128]{2,1,0:T(1,128)S(1)} %get-tuple-element.108), channel_id=1, source_target_pairs={{8,0},{16,8},{24,16},{9,1},{17,9},{25,17},{10,2},{18,10},{26,18},{... | collective-permute-start | bytes 98312 | tf_op jit(solution)/shard_map/ppermute | solution.py:25
  114.0 18.0 %collective-permute-start.19 = (f32[64,1,128]{2,1,0:T(1,128)S(1)}, f32[64,1,128]{2,1,0:T(1,128)S(1)}, u32[]{:S(2)}, u32[]{:S(2)}) collective-permute-start(f32[64,1,128]{2,1,0:T(1,128)S(1)} %get-tuple-element.109), channel_id=1, source_target_pairs={{0,8},{8,16},{16,24},{1,9},{9,17},{17,25},{2,10},{10,18},{18,26},{... | collective-permute-start | bytes 98312 | tf_op jit(solution)/shard_map/ppermute | solution.py:24
  118.7 13.3 %collective-permute-start.16 = (f32[64,8,1]{2,1,0:T(8,128)S(1)}, f32[64,8,1]{2,1,0:T(8,128)S(1)}, u32[]{:S(2)}, u32[]{:S(2)}) collective-permute-start(f32[64,8,1]{2,1,0:T(8,128)S(1)} %get-tuple-element.106), channel_id=1, source_target_pairs={{2,0},{4,2},{6,4},{0,6},{3,1},{5,3},{7,5},{1,7},{10,8},{12,10},{14... | collective-permute-start | bytes 6152 | tf_op jit(solution)/shard_map/ppermute | solution.py:25
  121.7 10.4 %collective-permute-start.17 = (f32[64,8,1]{2,1,0:T(8,128)S(1)}, f32[64,8,1]{2,1,0:T(8,128)S(1)}, u32[]{:S(2)}, u32[]{:S(2)}) collective-permute-start(f32[64,8,1]{2,1,0:T(8,128)S(1)} %get-tuple-element.107), channel_id=1, source_target_pairs={{0,2},{2,4},{4,6},{6,0},{1,3},{3,5},{5,7},{7,1},{8,10},{10,12},{12... | collective-permute-start | bytes 6152 | tf_op jit(solution)/shard_map/ppermute | solution.py:24
  139.8 16.6 %collective-permute-start.22 = (f32[64,10,1]{2,1,0:T(8,128)}, f32[64,10,1]{2,1,0:T(8,128)S(1)}, u32[]{:S(2)}, u32[]{:S(2)}) collective-permute-start(f32[64,10,1]{2,1,0:T(8,128)} %get-tuple-element.52), channel_id=1, source_target_pairs={{0,2},{2,4},{4,6},{6,0},{1,3},{3,5},{5,7},{7,1},{8,10},{10,12},{12... | collective-permute-start | bytes 7688 | tf_op jit(solution)/shard_map/ppermute | solution.py:24
  140.3 21.7 %collective-permute-start.23 = (f32[64,10,1]{2,1,0:T(8,128)}, f32[64,10,1]{2,1,0:T(8,128)}, u32[]{:S(2)}, u32[]{:S(2)}) collective-permute-start(f32[64,10,1]{2,1,0:T(8,128)} %get-tuple-element.53), channel_id=1, source_target_pairs={{2,0},{4,2},{6,4},{0,6},{3,1},{5,3},{7,5},{1,7},{10,8},{12,10},{14... | collective-permute-start | bytes 7688 | tf_op jit(solution)/shard_map/ppermute | solution.py:25
  144.3 89.1 %all-to-all-start.1 = ((f32[2,16,8]{2,0,1:T(2,128)}), f32[2,16,8]{2,0,1:T(2,128)}, u32[]{:S(2)}, u32[]{:S(2)}) async-start(f32[2,16,8]{2,0,1:T(2,128)} %bitcast.16), calls=%async_computation.1 | async-start | bytes 32768 | tf_op jit(solution)/shard_map/all_to_all | solution.py:98
  164.3 13.8 %collective-permute-start.24 = (f32[64,8,1]{2,1,0:T(8,128)S(1)}, f32[64,8,1]{2,1,0:T(8,128)S(1)}, u32[]{:S(2)}, u32[]{:S(2)}) collective-permute-start(f32[64,8,1]{2,1,0:T(8,128)S(1)} %get-tuple-element.100), channel_id=1, source_target_pairs={{2,0},{4,2},{6,4},{0,6},{3,1},{5,3},{7,5},{1,7},{10,8},{12,10},{14... | collective-permute-start | bytes 6152 | tf_op jit(solution)/shard_map/ppermute | solution.py:25
  167.2 10.9 %collective-permute-start.25 = (f32[64,8,1]{2,1,0:T(8,128)S(1)}, f32[64,8,1]{2,1,0:T(8,128)S(1)}, u32[]{:S(2)}, u32[]{:S(2)}) collective-permute-start(f32[64,8,1]{2,1,0:T(8,128)S(1)} %get-tuple-element.101), channel_id=1, source_target_pairs={{0,2},{2,4},{4,6},{6,0},{1,3},{3,5},{5,7},{7,1},{8,10},{10,12},{12... | collective-permute-start | bytes 6152 | tf_op jit(solution)/shard_map/ppermute | solution.py:24
  167.2 10.9 %collective-permute-start.26 = (f32[64,1,128]{2,1,0:T(1,128)S(1)}, f32[64,1,128]{2,1,0:T(1,128)S(1)}, u32[]{:S(2)}, u32[]{:S(2)}) collective-permute-start(f32[64,1,128]{2,1,0:T(1,128)S(1)} %get-tuple-element.102), channel_id=1, source_target_pairs={{8,0},{16,8},{24,16},{9,1},{17,9},{25,17},{10,2},{18,10},{26,18},{... | collective-permute-start | bytes 98312 | tf_op jit(solution)/shard_map/ppermute | solution.py:25
  184.2 16.6 %collective-permute-start.30 = (f32[64,10,1]{2,1,0:T(8,128)S(1)}, f32[64,10,1]{2,1,0:T(8,128)S(1)}, u32[]{:S(2)}, u32[]{:S(2)}) collective-permute-start(f32[64,10,1]{2,1,0:T(8,128)S(1)} %get-tuple-element.50), channel_id=1, source_target_pairs={{0,2},{2,4},{4,6},{6,0},{1,3},{3,5},{5,7},{7,1},{8,10},{10,12},{12... | collective-permute-start | bytes 7688 | tf_op jit(solution)/shard_map/ppermute | solution.py:24
  184.9 22.1 %collective-permute-start.31 = (f32[64,10,1]{2,1,0:T(8,128)S(1)}, f32[64,10,1]{2,1,0:T(8,128)S(1)}, u32[]{:S(2)}, u32[]{:S(2)}) collective-permute-start(f32[64,10,1]{2,1,0:T(8,128)S(1)} %get-tuple-element.51), channel_id=1, source_target_pairs={{2,0},{4,2},{6,4},{0,6},{3,1},{5,3},{7,5},{1,7},{10,8},{12,10},{14... | collective-permute-start | bytes 7688 | tf_op jit(solution)/shard_map/ppermute | solution.py:25
  208.2 13.9 %collective-permute-start.32 = (f32[64,8,1]{2,1,0:T(8,128)S(1)}, f32[64,8,1]{2,1,0:T(8,128)S(1)}, u32[]{:S(2)}, u32[]{:S(2)}) collective-permute-start(f32[64,8,1]{2,1,0:T(8,128)S(1)} %get-tuple-element.94), channel_id=1, source_target_pairs={{2,0},{4,2},{6,4},{0,6},{3,1},{5,3},{7,5},{1,7},{10,8},{12,10},{14... | collective-permute-start | bytes 6152 | tf_op jit(solution)/shard_map/ppermute | solution.py:25
  210.3 11.8 %collective-permute-start.33 = (f32[64,8,1]{2,1,0:T(8,128)S(1)}, f32[64,8,1]{2,1,0:T(8,128)S(1)}, u32[]{:S(2)}, u32[]{:S(2)}) collective-permute-start(f32[64,8,1]{2,1,0:T(8,128)S(1)} %get-tuple-element.95), channel_id=1, source_target_pairs={{0,2},{2,4},{4,6},{6,0},{1,3},{3,5},{5,7},{7,1},{8,10},{10,12},{12... | collective-permute-start | bytes 6152 | tf_op jit(solution)/shard_map/ppermute | solution.py:24
  210.4 11.7 %collective-permute-start.34 = (f32[64,1,128]{2,1,0:T(1,128)S(1)}, f32[64,1,128]{2,1,0:T(1,128)S(1)}, u32[]{:S(2)}, u32[]{:S(2)}) collective-permute-start(f32[64,1,128]{2,1,0:T(1,128)S(1)} %get-tuple-element.96), channel_id=1, source_target_pairs={{8,0},{16,8},{24,16},{9,1},{17,9},{25,17},{10,2},{18,10},{26,18},{... | collective-permute-start | bytes 98312 | tf_op jit(solution)/shard_map/ppermute | solution.py:25
  211.7 10.4 %collective-permute-start.35 = (f32[64,1,128]{2,1,0:T(1,128)S(1)}, f32[64,1,128]{2,1,0:T(1,128)S(1)}, u32[]{:S(2)}, u32[]{:S(2)}) collective-permute-start(f32[64,1,128]{2,1,0:T(1,128)S(1)} %get-tuple-element.97), channel_id=1, source_target_pairs={{0,8},{8,16},{16,24},{1,9},{9,17},{17,25},{2,10},{10,18},{18,26},{... | collective-permute-start | bytes 98312 | tf_op jit(solution)/shard_map/ppermute | solution.py:24
  229.6 16.8 %collective-permute-start.38 = (f32[64,10,1]{2,1,0:T(8,128)}, f32[64,10,1]{2,1,0:T(8,128)S(1)}, u32[]{:S(2)}, u32[]{:S(2)}) collective-permute-start(f32[64,10,1]{2,1,0:T(8,128)} %get-tuple-element.48), channel_id=1, source_target_pairs={{0,2},{2,4},{4,6},{6,0},{1,3},{3,5},{5,7},{7,1},{8,10},{10,12},{12... | collective-permute-start | bytes 7688 | tf_op jit(solution)/shard_map/ppermute | solution.py:24
  230.1 22.8 %collective-permute-start.39 = (f32[64,10,1]{2,1,0:T(8,128)S(1)}, f32[64,10,1]{2,1,0:T(8,128)}, u32[]{:S(2)}, u32[]{:S(2)}) collective-permute-start(f32[64,10,1]{2,1,0:T(8,128)S(1)} %get-tuple-element.49), channel_id=1, source_target_pairs={{2,0},{4,2},{6,4},{0,6},{3,1},{5,3},{7,5},{1,7},{10,8},{12,10},{14... | collective-permute-start | bytes 7688 | tf_op jit(solution)/shard_map/ppermute | solution.py:25
  233.4 31.0 %all-to-all-start = ((f32[2,16,8]{2,0,1:T(2,128)}), f32[2,16,8]{2,0,1:T(2,128)}, u32[]{:S(2)}, u32[]{:S(2)}) async-start(f32[2,16,8]{2,0,1:T(2,128)} %bitcast.208), calls=%async_computation | async-start | bytes 32768 | tf_op jit(solution)/shard_map/all_to_all | solution.py:99
  237.5 145.2 %all-reduce.7.cloned.1.call-start = ((), (), s32[]{:S(2)}) async-start(), calls=%async_computation.5 | async-start | bytes 262144 | tf_op jit(solution)/shard_map/psum | solution.py:115
  255.2 13.8 %collective-permute-start.40 = (f32[64,8,1]{2,1,0:T(8,128)S(1)}, f32[64,8,1]{2,1,0:T(8,128)S(1)}, u32[]{:S(2)}, u32[]{:S(2)}) collective-permute-start(f32[64,8,1]{2,1,0:T(8,128)S(1)} %get-tuple-element.88), channel_id=1, source_target_pairs={{2,0},{4,2},{6,4},{0,6},{3,1},{5,3},{7,5},{1,7},{10,8},{12,10},{14... | collective-permute-start | bytes 6152 | tf_op jit(solution)/shard_map/ppermute | solution.py:25
  257.3 11.7 %collective-permute-start.41 = (f32[64,8,1]{2,1,0:T(8,128)S(1)}, f32[64,8,1]{2,1,0:T(8,128)S(1)}, u32[]{:S(2)}, u32[]{:S(2)}) collective-permute-start(f32[64,8,1]{2,1,0:T(8,128)S(1)} %get-tuple-element.89), channel_id=1, source_target_pairs={{0,2},{2,4},{4,6},{6,0},{1,3},{3,5},{5,7},{7,1},{8,10},{10,12},{12... | collective-permute-start | bytes 6152 | tf_op jit(solution)/shard_map/ppermute | solution.py:24
  258.0 11.1 %collective-permute-start.42 = (f32[64,1,128]{2,1,0:T(1,128)}, f32[64,1,128]{2,1,0:T(1,128)}, u32[]{:S(2)}, u32[]{:S(2)}) collective-permute-start(f32[64,1,128]{2,1,0:T(1,128)} %get-tuple-element.90), channel_id=1, source_target_pairs={{8,0},{16,8},{24,16},{9,1},{17,9},{25,17},{10,2},{18,10},{26,18},{... | collective-permute-start | bytes 98312 | tf_op jit(solution)/shard_map/ppermute | solution.py:25
  277.4 130.6 %all-gather.3.cloned.1.call-start = ((), (), s32[]{:S(2)}) async-start(), calls=%async_computation.2 | async-start | bytes 1572864 | tf_op jit(solution)/shard_map/all_gather | solution.py:123
  278.0 485.0 %all-reduce.5.cloned.1.call-start = ((), (), s32[]{:S(2)}) async-start(), calls=%async_computation.4 | async-start | bytes 262144 | tf_op jit(solution)/shard_map/psum | solution.py:115
  417.3 16.6 %collective-permute-start.46 = (f32[64,10,1]{2,1,0:T(8,128)S(1)}, f32[64,10,1]{2,1,0:T(8,128)S(1)}, u32[]{:S(2)}, u32[]{:S(2)}) collective-permute-start(f32[64,10,1]{2,1,0:T(8,128)S(1)} %get-tuple-element.44), channel_id=1, source_target_pairs={{0,2},{2,4},{4,6},{6,0},{1,3},{3,5},{5,7},{7,1},{8,10},{10,12},{12... | collective-permute-start | bytes 7688 | tf_op jit(solution)/shard_map/ppermute | solution.py:24
  418.1 21.4 %collective-permute-start.47 = (f32[64,10,1]{2,1,0:T(8,128)S(1)}, f32[64,10,1]{2,1,0:T(8,128)S(1)}, u32[]{:S(2)}, u32[]{:S(2)}) collective-permute-start(f32[64,10,1]{2,1,0:T(8,128)S(1)} %get-tuple-element.45), channel_id=1, source_target_pairs={{2,0},{4,2},{6,4},{0,6},{3,1},{5,3},{7,5},{1,7},{10,8},{12,10},{14... | collective-permute-start | bytes 7688 | tf_op jit(solution)/shard_map/ppermute | solution.py:25
  440.6 18.8 %collective-permute-start.50 = (f32[64,1,128]{2,1,0:T(1,128)S(1)}, f32[64,1,128]{2,1,0:T(1,128)S(1)}, u32[]{:S(2)}, u32[]{:S(2)}) collective-permute-start(f32[64,1,128]{2,1,0:T(1,128)S(1)} %get-tuple-element.84), channel_id=1, source_target_pairs={{8,0},{16,8},{24,16},{9,1},{17,9},{25,17},{10,2},{18,10},{26,18},{... | collective-permute-start | bytes 98312 | tf_op jit(solution)/shard_map/ppermute | solution.py:25
  441.9 17.6 %collective-permute-start.51 = (f32[64,1,128]{2,1,0:T(1,128)S(1)}, f32[64,1,128]{2,1,0:T(1,128)S(1)}, u32[]{:S(2)}, u32[]{:S(2)}) collective-permute-start(f32[64,1,128]{2,1,0:T(1,128)S(1)} %get-tuple-element.85), channel_id=1, source_target_pairs={{0,8},{8,16},{16,24},{1,9},{9,17},{17,25},{2,10},{10,18},{18,26},{... | collective-permute-start | bytes 98312 | tf_op jit(solution)/shard_map/ppermute | solution.py:24
  446.8 12.6 %collective-permute-start.48 = (f32[64,8,1]{2,1,0:T(8,128)S(1)}, f32[64,8,1]{2,1,0:T(8,128)S(1)}, u32[]{:S(2)}, u32[]{:S(2)}) collective-permute-start(f32[64,8,1]{2,1,0:T(8,128)S(1)} %get-tuple-element.82), channel_id=1, source_target_pairs={{2,0},{4,2},{6,4},{0,6},{3,1},{5,3},{7,5},{1,7},{10,8},{12,10},{14... | collective-permute-start | bytes 6152 | tf_op jit(solution)/shard_map/ppermute | solution.py:25
  449.0 10.4 %collective-permute-start.49 = (f32[64,8,1]{2,1,0:T(8,128)S(1)}, f32[64,8,1]{2,1,0:T(8,128)S(1)}, u32[]{:S(2)}, u32[]{:S(2)}) collective-permute-start(f32[64,8,1]{2,1,0:T(8,128)S(1)} %get-tuple-element.83), channel_id=1, source_target_pairs={{0,2},{2,4},{4,6},{6,0},{1,3},{3,5},{5,7},{7,1},{8,10},{10,12},{12... | collective-permute-start | bytes 6152 | tf_op jit(solution)/shard_map/ppermute | solution.py:24
  466.9 16.6 %collective-permute-start.54 = (f32[64,10,1]{2,1,0:T(8,128)S(1)}, f32[64,10,1]{2,1,0:T(8,128)S(1)}, u32[]{:S(2)}, u32[]{:S(2)}) collective-permute-start(f32[64,10,1]{2,1,0:T(8,128)S(1)} %get-tuple-element.42), channel_id=1, source_target_pairs={{0,2},{2,4},{4,6},{6,0},{1,3},{3,5},{5,7},{7,1},{8,10},{10,12},{12... | collective-permute-start | bytes 7688 | tf_op jit(solution)/shard_map/ppermute | solution.py:24
  468.3 21.6 %collective-permute-start.55 = (f32[64,10,1]{2,1,0:T(8,128)S(1)}, f32[64,10,1]{2,1,0:T(8,128)S(1)}, u32[]{:S(2)}, u32[]{:S(2)}) collective-permute-start(f32[64,10,1]{2,1,0:T(8,128)S(1)} %get-tuple-element.43), channel_id=1, source_target_pairs={{2,0},{4,2},{6,4},{0,6},{3,1},{5,3},{7,5},{1,7},{10,8},{12,10},{14... | collective-permute-start | bytes 7688 | tf_op jit(solution)/shard_map/ppermute | solution.py:25
  491.0 19.2 %collective-permute-start.58 = (f32[64,1,128]{2,1,0:T(1,128)S(1)}, f32[64,1,128]{2,1,0:T(1,128)S(1)}, u32[]{:S(2)}, u32[]{:S(2)}) collective-permute-start(f32[64,1,128]{2,1,0:T(1,128)S(1)} %get-tuple-element.78), channel_id=1, source_target_pairs={{8,0},{16,8},{24,16},{9,1},{17,9},{25,17},{10,2},{18,10},{26,18},{... | collective-permute-start | bytes 98312 | tf_op jit(solution)/shard_map/ppermute | solution.py:25
  492.3 17.9 %collective-permute-start.59 = (f32[64,1,128]{2,1,0:T(1,128)S(1)}, f32[64,1,128]{2,1,0:T(1,128)S(1)}, u32[]{:S(2)}, u32[]{:S(2)}) collective-permute-start(f32[64,1,128]{2,1,0:T(1,128)S(1)} %get-tuple-element.79), channel_id=1, source_target_pairs={{0,8},{8,16},{16,24},{1,9},{9,17},{17,25},{2,10},{10,18},{18,26},{... | collective-permute-start | bytes 98312 | tf_op jit(solution)/shard_map/ppermute | solution.py:24
  499.6 10.6 %collective-permute-start.57 = (f32[64,8,1]{2,1,0:T(8,128)S(1)}, f32[64,8,1]{2,1,0:T(8,128)S(1)}, u32[]{:S(2)}, u32[]{:S(2)}) collective-permute-start(f32[64,8,1]{2,1,0:T(8,128)S(1)} %get-tuple-element.77), channel_id=1, source_target_pairs={{0,2},{2,4},{4,6},{6,0},{1,3},{3,5},{5,7},{7,1},{8,10},{10,12},{12... | collective-permute-start | bytes 6152 | tf_op jit(solution)/shard_map/ppermute | solution.py:24
  516.8 16.6 %collective-permute-start.62 = (f32[64,10,1]{2,1,0:T(8,128)S(1)}, f32[64,10,1]{2,1,0:T(8,128)S(1)}, u32[]{:S(2)}, u32[]{:S(2)}) collective-permute-start(f32[64,10,1]{2,1,0:T(8,128)S(1)} %get-tuple-element.40), channel_id=1, source_target_pairs={{0,2},{2,4},{4,6},{6,0},{1,3},{3,5},{5,7},{7,1},{8,10},{10,12},{12... | collective-permute-start | bytes 7688 | tf_op jit(solution)/shard_map/ppermute | solution.py:24
  518.3 20.8 %collective-permute-start.63 = (f32[64,10,1]{2,1,0:T(8,128)S(1)}, f32[64,10,1]{2,1,0:T(8,128)S(1)}, u32[]{:S(2)}, u32[]{:S(2)}) collective-permute-start(f32[64,10,1]{2,1,0:T(8,128)S(1)} %get-tuple-element.41), channel_id=1, source_target_pairs={{2,0},{4,2},{6,4},{0,6},{3,1},{5,3},{7,5},{1,7},{10,8},{12,10},{14... | collective-permute-start | bytes 7688 | tf_op jit(solution)/shard_map/ppermute | solution.py:25
  540.3 19.9 %collective-permute-start.66 = (f32[64,1,128]{2,1,0:T(1,128)S(1)}, f32[64,1,128]{2,1,0:T(1,128)S(1)}, u32[]{:S(2)}, u32[]{:S(2)}) collective-permute-start(f32[64,1,128]{2,1,0:T(1,128)S(1)} %get-tuple-element.72), channel_id=1, source_target_pairs={{8,0},{16,8},{24,16},{9,1},{17,9},{25,17},{10,2},{18,10},{26,18},{... | collective-permute-start | bytes 98312 | tf_op jit(solution)/shard_map/ppermute | solution.py:25
  541.6 18.6 %collective-permute-start.67 = (f32[64,1,128]{2,1,0:T(1,128)S(1)}, f32[64,1,128]{2,1,0:T(1,128)S(1)}, u32[]{:S(2)}, u32[]{:S(2)}) collective-permute-start(f32[64,1,128]{2,1,0:T(1,128)S(1)} %get-tuple-element.73), channel_id=1, source_target_pairs={{0,8},{8,16},{16,24},{1,9},{9,17},{17,25},{2,10},{10,18},{18,26},{... | collective-permute-start | bytes 98312 | tf_op jit(solution)/shard_map/ppermute | solution.py:24
  546.3 10.4 %collective-permute-start.64 = (f32[64,8,1]{2,1,0:T(8,128)S(1)}, f32[64,8,1]{2,1,0:T(8,128)S(1)}, u32[]{:S(2)}, u32[]{:S(2)}) collective-permute-start(f32[64,8,1]{2,1,0:T(8,128)S(1)} %get-tuple-element.70), channel_id=1, source_target_pairs={{2,0},{4,2},{6,4},{0,6},{3,1},{5,3},{7,5},{1,7},{10,8},{12,10},{14... | collective-permute-start | bytes 6152 | tf_op jit(solution)/shard_map/ppermute | solution.py:25
  549.6 10.6 %collective-permute-start.65 = (f32[64,8,1]{2,1,0:T(8,128)S(1)}, f32[64,8,1]{2,1,0:T(8,128)S(1)}, u32[]{:S(2)}, u32[]{:S(2)}) collective-permute-start(f32[64,8,1]{2,1,0:T(8,128)S(1)} %get-tuple-element.71), channel_id=1, source_target_pairs={{0,2},{2,4},{4,6},{6,0},{1,3},{3,5},{5,7},{7,1},{8,10},{10,12},{12... | collective-permute-start | bytes 6152 | tf_op jit(solution)/shard_map/ppermute | solution.py:24
  566.8 16.6 %collective-permute-start.70 = (f32[64,10,1]{2,1,0:T(8,128)S(1)}, f32[64,10,1]{2,1,0:T(8,128)S(1)}, u32[]{:S(2)}, u32[]{:S(2)}) collective-permute-start(f32[64,10,1]{2,1,0:T(8,128)S(1)} %get-tuple-element.38), channel_id=1, source_target_pairs={{0,2},{2,4},{4,6},{6,0},{1,3},{3,5},{5,7},{7,1},{8,10},{10,12},{12... | collective-permute-start | bytes 7688 | tf_op jit(solution)/shard_map/ppermute | solution.py:24
  568.3 19.6 %collective-permute-start.71 = (f32[64,10,1]{2,1,0:T(8,128)S(1)}, f32[64,10,1]{2,1,0:T(8,128)S(1)}, u32[]{:S(2)}, u32[]{:S(2)}) collective-permute-start(f32[64,10,1]{2,1,0:T(8,128)S(1)} %get-tuple-element.39), channel_id=1, source_target_pairs={{2,0},{4,2},{6,4},{0,6},{3,1},{5,3},{7,5},{1,7},{10,8},{12,10},{14... | collective-permute-start | bytes 7688 | tf_op jit(solution)/shard_map/ppermute | solution.py:25
  589.1 19.0 %collective-permute-start.74 = (f32[64,1,128]{2,1,0:T(1,128)S(1)}, f32[64,1,128]{2,1,0:T(1,128)S(1)}, u32[]{:S(2)}, u32[]{:S(2)}) collective-permute-start(f32[64,1,128]{2,1,0:T(1,128)S(1)} %get-tuple-element.66), channel_id=1, source_target_pairs={{8,0},{16,8},{24,16},{9,1},{17,9},{25,17},{10,2},{18,10},{26,18},{... | collective-permute-start | bytes 98312 | tf_op jit(solution)/shard_map/ppermute | solution.py:25
  590.4 17.7 %collective-permute-start.75 = (f32[64,1,128]{2,1,0:T(1,128)S(1)}, f32[64,1,128]{2,1,0:T(1,128)S(1)}, u32[]{:S(2)}, u32[]{:S(2)}) collective-permute-start(f32[64,1,128]{2,1,0:T(1,128)S(1)} %get-tuple-element.67), channel_id=1, source_target_pairs={{0,8},{8,16},{16,24},{1,9},{9,17},{17,25},{2,10},{10,18},{18,26},{... | collective-permute-start | bytes 98312 | tf_op jit(solution)/shard_map/ppermute | solution.py:24
  597.8 10.3 %collective-permute-start.73 = (f32[64,8,1]{2,1,0:T(8,128)S(1)}, f32[64,8,1]{2,1,0:T(8,128)S(1)}, u32[]{:S(2)}, u32[]{:S(2)}) collective-permute-start(f32[64,8,1]{2,1,0:T(8,128)S(1)} %get-tuple-element.65), channel_id=1, source_target_pairs={{0,2},{2,4},{4,6},{6,0},{1,3},{3,5},{5,7},{7,1},{8,10},{10,12},{12... | collective-permute-start | bytes 6152 | tf_op jit(solution)/shard_map/ppermute | solution.py:24
  614.5 15.7 %collective-permute-start.78 = (f32[64,10,1]{2,1,0:T(8,128)S(1)}, f32[64,10,1]{2,1,0:T(8,128)S(1)}, u32[]{:S(2)}, u32[]{:S(2)}) collective-permute-start(f32[64,10,1]{2,1,0:T(8,128)S(1)} %get-tuple-element.36), channel_id=1, source_target_pairs={{0,2},{2,4},{4,6},{6,0},{1,3},{3,5},{5,7},{7,1},{8,10},{10,12},{12... | collective-permute-start | bytes 7688 | tf_op jit(solution)/shard_map/ppermute | solution.py:24
  616.0 19.2 %collective-permute-start.79 = (f32[64,10,1]{2,1,0:T(8,128)S(1)}, f32[64,10,1]{2,1,0:T(8,128)S(1)}, u32[]{:S(2)}, u32[]{:S(2)}) collective-permute-start(f32[64,10,1]{2,1,0:T(8,128)S(1)} %get-tuple-element.37), channel_id=1, source_target_pairs={{2,0},{4,2},{6,4},{0,6},{3,1},{5,3},{7,5},{1,7},{10,8},{12,10},{14... | collective-permute-start | bytes 7688 | tf_op jit(solution)/shard_map/ppermute | solution.py:25
  638.8 11.1 %collective-permute-start.81 = (f32[64,8,1]{2,1,0:T(8,128)S(1)}, f32[64,8,1]{2,1,0:T(8,128)S(1)}, u32[]{:S(2)}, u32[]{:S(2)}) collective-permute-start(f32[64,8,1]{2,1,0:T(8,128)S(1)} %get-tuple-element.59), channel_id=1, source_target_pairs={{0,2},{2,4},{4,6},{6,0},{1,3},{3,5},{5,7},{7,1},{8,10},{10,12},{12... | collective-permute-start | bytes 6152 | tf_op jit(solution)/shard_map/ppermute | solution.py:24
  638.8 11.0 %collective-permute-start.82 = (f32[64,1,128]{2,1,0:T(1,128)S(1)}, f32[64,1,128]{2,1,0:T(1,128)S(1)}, u32[]{:S(2)}, u32[]{:S(2)}) collective-permute-start(f32[64,1,128]{2,1,0:T(1,128)S(1)} %get-tuple-element.60), channel_id=1, source_target_pairs={{8,0},{16,8},{24,16},{9,1},{17,9},{25,17},{10,2},{18,10},{26,18},{... | collective-permute-start | bytes 98312 | tf_op jit(solution)/shard_map/ppermute | solution.py:25
  657.3 131.0 %all-gather.5.cloned.1.call-start = ((), (), s32[]{:S(2)}) async-start(), calls=%async_computation.3 | async-start | bytes 1572864 | tf_op jit(solution)/shard_map/all_gather | solution.py:123
  (53 other events, 585.8 us)
Sparse Core Ops, SparseCore 0:
  277.5 105.1 all-reduce.6
  657.4 105.5 all-reduce.4
Sparse Core Ops, SparseCore 1:
  279.4 8.2 all-gather.2
  659.3 8.7 all-gather.4
where the time goes:
time: 810 us; the launch traced here: 800 us
  waiting for transfers between devices  505 us (62%)
  starting transfers between devices  173 us (21%)
  other arithmetic  69.1 us (9%)
  local copies, waits for them, and re-layouts  25.9 us (3%)
  between operations  16.3 us (2%)
    psum x2, waiting for transfers between devices, per_device(): gram_part, cross_part = lax.psum((gram_part, cross_part), ('lat', 'lon'))  210 us
    ppermute x42, waiting for transfers between devices, padded_2(): before = lax.ppermute(last, axis, up)  150 us
    ppermute x42, waiting for transfers between devices, padded_2(): after = lax.ppermute(leading, axis, down)  144 us
    ppermute x42, starting transfers between devices, padded_2(): before = lax.ppermute(last, axis, up)  83.1 us
    ppermute x42, starting transfers between devices, padded_2(): after = lax.ppermute(leading, axis, down)  81.5 us
    another operation x6, other arithmetic, solve_weights(): factor = jnp.linalg.cholesky(system)  24.8 us
    another operation x4, other arithmetic, solve_weights(): jax.scipy.linalg.cho_solve((factor, True), cross_part) / math.sqrt(members)  21 us
  transfers between devices with their start and end apart: 90, of which 57 were waited for; matrix products, arithmetic and copies ran while one was open for 8% of the time, Pallas kernels for 0%

commit v1 on v0

--- a/solution.py
+++ b/solution.py
@@ -1,8 +1,12 @@
 import math
+
+import functools
 
 import jax
 import jax.numpy as jnp
 from jax import lax
+from jax.experimental import pallas as pl
+from jax.experimental.pallas import tpu as pltpu
 from jax.sharding import PartitionSpec as P
 
 STEPS = 6
@@ -89,7 +93,7 @@
     return weights - jnp.mean(weights, axis=0, keepdims=True)
 
 
-def per_device(parameters, initial_height, initial_speed, obs_slots, obs_values, obs_precision):
+def per_device_halo(parameters, initial_height, initial_speed, obs_slots, obs_values, obs_precision):
     owners = obs_slots.shape[2]
     slot_count = obs_slots.shape[3]
     members_here = parameters.shape[1]
@@ -129,6 +133,413 @@
     return parameters
 
 
+MESH = pl.DeviceIdType.MESH
+VMEM = pltpu.VMEM
+
+
+def east(field):
+    width = field.shape[1]
+    return pltpu.roll(field, width - 1, 1) - pltpu.roll(field, 1, 1)
+
+
+def north(field, first_row, last_row):
+    height = field.shape[0]
+    after = jnp.where(last_row, 0.0, pltpu.roll(field, height - 1, 0))
+    before = jnp.where(first_row, 0.0, pltpu.roll(field, 1, 0))
+    return after - before
+
+
+def run_member(height, speed_e, speed_n, friction, forcing):
+    rows = lax.broadcasted_iota(jnp.int32, height.shape, 0)
+    first_row, last_row = (rows == 0, rows == height.shape[0] - 1)
+    keep = 1.0 - friction
+    for substep in range(STEPS):
+        flow = east(speed_e) + north(speed_n, first_row, last_row)
+        height = height - depth_step * flow + forcing
+        if substep < STEPS - 1:
+            speed_e, speed_n = (
+                keep * speed_e - gravity_step * east(height) + coriolis * speed_n,
+                keep * speed_n
+                - gravity_step * north(height, first_row, last_row)
+                - coriolis * speed_e,
+            )
+    return height
+
+
+def gather_kernel(iteration, n_lat, n_lon, n_ens, *refs):
+    first = iteration == 0
+    blocks = n_lat * n_lon
+    if first:
+        params, aux, gram, cross, other, full, got, send_a, recv_a = refs[:9]
+        refs = refs[9:]
+    else:
+        params, full, gram, cross, other, got = refs[:6]
+        refs = refs[6:]
+    (field, outgoing, arrived, part, pieces, summed, total) = refs[:7]
+    (send_p, recv_p, send_o, recv_o, send_y, recv_y, send_r, recv_r, send_t, recv_t) = refs[7:]
+    lat, lon, ens = (lax.axis_index("lat"), lax.axis_index("lon"), lax.axis_index("ens"))
+    me = lat * n_lon + lon
+    here = ens * blocks + me
+    everyone = blocks * n_ens
+    mine = params.shape[1] // blocks
+    rows, cols = params.shape[2:]
+
+    def peer(block):
+        return {"lat": block // n_lon, "lon": lax.rem(block, n_lon), "ens": ens}
+
+    def anyone(flat):
+        block = lax.rem(flat, blocks)
+        return {"lat": block // n_lon, "lon": lax.rem(block, n_lon), "ens": flat // blocks}
+
+    def each(count, body):
+        def step(i, carry):
+            body(i)
+            return carry
+
+        lax.fori_loop(1, count, step, 0)
+
+    def send(src, dst, send_sem, recv_sem, device):
+        return pltpu.make_async_remote_copy(
+            src_ref=src,
+            dst_ref=dst,
+            send_sem=send_sem,
+            recv_sem=recv_sem,
+            device_id=device,
+            device_id_type=MESH,
+        )
+
+    barrier = pltpu.get_barrier_semaphore()
+
+    def greet(i):
+        pl.semaphore_signal(
+            barrier, inc=1, device_id=anyone(lax.rem(here + i, everyone)), device_id_type=MESH
+        )
+
+    each(everyone, greet)
+    pl.semaphore_wait(barrier, everyone - 1)
+
+    def param_copy(i):
+        to = lax.rem(me + i, blocks)
+        return send(
+            params.at[:, pl.ds(to * mine, mine)], got.at[me], send_p.at[i], recv_p.at[i], peer(to)
+        )
+
+    def aux_copy(i):
+        to = lax.rem(me + i, blocks)
+        return send(aux, full.at[me], send_a.at[i], recv_a.at[i], peer(to))
+
+    def start_params(i):
+        if first:
+            aux_copy(i).start()
+        param_copy(i).start()
+
+    each(blocks, start_params)
+
+    def swap_copy(i):
+        return send(
+            params, other.at[0], send_o.at[0], recv_o.at[0], {"lat": lat, "lon": lon, "ens": 1 - ens}
+        )
+
+    swap_copy(0).start()
+    got[me] = params[:, pl.ds(me * mine, mine)]
+    if first:
+        full[me] = aux[...]
+
+    def end_params(i):
+        if first:
+            aux_copy(i).wait()
+        param_copy(i).wait()
+
+    each(blocks, end_params)
+
+    def whole(pick):
+        lines = []
+        for a in range(n_lat):
+            lines.append(jnp.concatenate([pick(a * n_lon + b) for b in range(n_lon)], axis=1))
+        return jnp.concatenate(lines, axis=0)
+
+    def member(j, carry):
+        height = run_member(
+            whole(lambda b: full[b, 0]),
+            whole(lambda b: full[b, 1]),
+            whole(lambda b: full[b, 2]),
+            whole(lambda b: got[b, 0, j]),
+            whole(lambda b: got[b, 1, j]),
+        )
+        for a in range(n_lat):
+            for b in range(n_lon):
+                field[a * n_lon + b, j] = height[
+                    a * rows : (a + 1) * rows, b * cols : (b + 1) * cols
+                ]
+        return carry
+
+    lax.fori_loop(0, mine, member, 0)
+
+    row_ids = lax.broadcasted_iota(jnp.int32, (rows, cols), 0)
+
+    def pick_block(b, carry):
+        cells = full[b, 3][iteration : iteration + 1].astype(jnp.int32)
+        cells = jnp.broadcast_to(cells, (rows, cols))
+        lanes = jnp.bitwise_and(cells, cols - 1)
+        hit = row_ids == jnp.right_shift(cells, cols.bit_length() - 1)
+        found = jnp.zeros((rows, cols), jnp.float32)
+        for j in range(mine):
+            tile = jnp.take_along_axis(field[b, j], lanes, axis=1)
+            value = jnp.sum(jnp.where(hit, tile, 0.0), axis=0, keepdims=True)
+            found = jnp.where(row_ids == j, value, found)
+        outgoing[b] = found
+        return carry
+
+    lax.fori_loop(0, blocks, pick_block, 0)
+
+    def answer_copy(i):
+        to = lax.rem(here + i, everyone)
+        return send(
+            outgoing.at[lax.rem(to, blocks)],
+            arrived.at[here],
+            send_y.at[i],
+            recv_y.at[i],
+            anyone(to),
+        )
+
+    each(everyone, lambda i: answer_copy(i).start())
+    arrived[here] = outgoing[me]
+
+    slots = full.shape[-1] // blocks
+    heard = jnp.concatenate([full[b, 3] for b in range(blocks)], axis=0)
+    kinds = full.shape[2]
+    lane_ids = lax.broadcasted_iota(jnp.int32, heard.shape, 1)
+    line_ids = lax.broadcasted_iota(jnp.int32, heard.shape, 0)
+    square = (heard.shape[1], heard.shape[1])
+    from_ids = lax.broadcasted_iota(jnp.int32, square, 0)
+    to_ids = lax.broadcasted_iota(jnp.int32, square, 1)
+    chosen = from_ids == me * slots + lax.rem(to_ids, slots)
+    spread_out = jnp.dot(
+        heard,
+        chosen.astype(jnp.float32),
+        precision=lax.Precision.HIGHEST,
+        preferred_element_type=jnp.float32,
+    )
+
+    def of_kind(kind):
+        wanted = line_ids == (lane_ids // slots) * kinds + kind
+        return jnp.sum(jnp.where(wanted, spread_out, 0.0), axis=0, keepdims=True)
+
+    observed = of_kind(2 + iteration)
+    precision = of_kind(4 + iteration)
+
+    each(everyone, lambda i: answer_copy(i).wait())
+
+    predicted = jnp.concatenate([arrived[s][:mine] for s in range(everyone)], axis=0)
+    members = predicted.shape[0]
+    spread = predicted - jnp.sum(predicted, axis=0, keepdims=True) / members
+    weighted = spread * precision
+    is_gram = ens == 0
+    right = jnp.where(is_gram, spread, observed - predicted)
+    scale = jnp.where(is_gram, 1.0 / members, 1.0 / math.sqrt(members))
+    product = lax.dot_general(
+        weighted,
+        right,
+        (((1,), (1,)), ((), ())),
+        precision=lax.Precision.HIGHEST,
+        preferred_element_type=jnp.float32,
+    )
+    product = product * scale
+    lines = members // blocks
+    for b in range(blocks):
+        part[b] = product[b * lines : (b + 1) * lines]
+
+    def piece_copy(i):
+        to = lax.rem(me + i, blocks)
+        return send(part.at[to], pieces.at[me], send_r.at[i], recv_r.at[i], peer(to))
+
+    each(blocks, lambda i: piece_copy(i).start())
+    pieces[me] = part[me]
+    each(blocks, lambda i: piece_copy(i).wait())
+    line = pieces[0]
+    for b in range(1, blocks):
+        line = line + pieces[b]
+    summed[...] = line
+
+    def total_copy(i):
+        to = lax.rem(here + i, everyone)
+        return send(summed, total.at[here], send_t.at[i], recv_t.at[i], anyone(to))
+
+    each(everyone, lambda i: total_copy(i).start())
+    total[here] = line
+    each(everyone, lambda i: total_copy(i).wait())
+    for b in range(blocks):
+        gram[b * lines : (b + 1) * lines, :] = total[b]
+        cross[b * lines : (b + 1) * lines, :] = total[blocks + b]
+    swap_copy(0).wait()
+
+
+def gather_call(iteration, sizes, params, extra):
+    n_lat, n_lon, n_ens = sizes
+    blocks = n_lat * n_lon
+    everyone = blocks * n_ens
+    members_here, rows, cols = params.shape[1:]
+    members = members_here * n_ens
+    mine = members_here // blocks
+    lines = members // blocks
+    f32 = jnp.float32
+    dma = pltpu.SemaphoreType.DMA
+    first = iteration == 0
+    outs = [
+        jax.ShapeDtypeStruct((members, members), f32),
+        jax.ShapeDtypeStruct((members, members), f32),
+        jax.ShapeDtypeStruct((1,) + params.shape, f32),
+    ]
+    scratch = [
+        VMEM((blocks, 2, mine, rows, cols), f32),
+    ]
+    if first:
+        outs.append(jax.ShapeDtypeStruct((blocks,) + extra.shape, f32))
+        scratch += [dma((blocks,)), dma((blocks,))]
+    scratch += [
+        VMEM((blocks, mine, rows, cols), f32),
+        VMEM((blocks, rows, cols), f32),
+        VMEM((everyone, rows, cols), f32),
+        VMEM((blocks, lines, members), f32),
+        VMEM((blocks, lines, members), f32),
+        VMEM((lines, members), f32),
+        VMEM((everyone, lines, members), f32),
+        dma((blocks,)),
+        dma((blocks,)),
+        dma((1,)),
+        dma((1,)),
+        dma((everyone,)),
+        dma((everyone,)),
+        dma((blocks,)),
+        dma((blocks,)),
+        dma((everyone,)),
+        dma((everyone,)),
+    ]
+    return pl.pallas_call(
+        functools.partial(gather_kernel, iteration, n_lat, n_lon, n_ens),
+        out_shape=outs,
+        in_specs=[pl.BlockSpec(memory_space=VMEM)] * 2,
+        out_specs=[pl.BlockSpec(memory_space=VMEM)] * len(outs),
+        scratch_shapes=scratch,
+        compiler_params=pltpu.CompilerParams(
+            collective_id=iteration, has_side_effects=True, vmem_limit_bytes=40 * 2**20
+        ),
+    )(params, extra)
+
+
+def with_rows(value, rows, start):
+    end = start + rows.shape[0]
+    pieces = [value[:start]] if start else []
+    pieces.append(rows)
+    if end < value.shape[0]:
+        pieces.append(value[end:])
+    return jnp.concatenate(pieces, axis=0)
+
+
+def eliminate(left, right):
+    size = left.shape[0]
+    panel = 8
+    row_ids = lax.broadcasted_iota(jnp.int32, (panel, size), 0)
+    for start in range(0, size, panel):
+        end = start + panel
+        rows_left, rows_right = (left[start:end], right[start:end])
+        columns = [
+            jnp.broadcast_to(rows_left[:, start + k : start + k + 1], (panel, size))
+            for k in range(panel)
+        ]
+        for k in range(panel):
+            column = columns[k]
+            inverse = 1.0 / column[k : k + 1]
+            here = row_ids == k
+
+            def reduce(value):
+                pivot_row = value[k : k + 1] * inverse
+                return jnp.where(here, pivot_row, value - column * pivot_row)
+
+            rows_left, rows_right = (reduce(rows_left), reduce(rows_right))
+            for later in range(k + 1, panel):
+                columns[later] = reduce(columns[later])
+        next_left, next_right = (left, right)
+        for k in range(panel):
+            column = left[:, start + k : start + k + 1]
+            next_left = next_left - column * rows_left[k : k + 1]
+            next_right = next_right - column * rows_right[k : k + 1]
+        left = with_rows(next_left, rows_left, start)
+        right = with_rows(next_right, rows_right, start)
+    return right
+
+
+def update_kernel(gram, cross, params, other, out):
+    ens = lax.axis_index("ens")
+    members = gram.shape[0]
+    members_here = params.shape[1]
+    ids = [lax.broadcasted_iota(jnp.int32, gram.shape, axis) for axis in (0, 1)]
+    system = gram[...] + (ids[0] == ids[1]).astype(jnp.float32)
+    weights = eliminate(system, cross[...]) / math.sqrt(members)
+    centred = weights - jnp.sum(weights, axis=0, keepdims=True) / members
+    turned = centred.T
+    mine = jnp.where(ens == 0, turned[:members_here], turned[members_here:])
+    mine = jnp.where(ens == 0, mine, pltpu.roll(mine, members_here, 1))
+    for p in range(params.shape[0]):
+        for r in range(params.shape[2]):
+            local = params[p, :, r, :]
+            stacked = jnp.concatenate([local, other[0, p, :, r, :]], axis=0)
+            out[p, :, r, :] = local + jnp.dot(
+                mine,
+                stacked,
+                precision=lax.Precision.HIGHEST,
+                preferred_element_type=jnp.float32,
+            )
+
+
+def update_call(gram, cross, params, other):
+    return pl.pallas_call(
+        update_kernel,
+        out_shape=jax.ShapeDtypeStruct(params.shape, jnp.float32),
+        in_specs=[pl.BlockSpec(memory_space=VMEM)] * 4,
+        out_specs=pl.BlockSpec(memory_space=VMEM),
+        compiler_params=pltpu.CompilerParams(vmem_limit_bytes=40 * 2**20),
+    )(gram, cross, params, other)
+
+
+def per_device_members(
+    sizes, parameters, initial_height, initial_speed, obs_slots, obs_values, obs_precision
+):
+    rows, cols = initial_height.shape
+    lines = [
+        v.reshape(ITERS, cols).astype(jnp.float32) for v in (obs_slots, obs_values, obs_precision)
+    ]
+    lines.append(jnp.zeros((rows - 3 * ITERS, cols), jnp.float32))
+    aux = jnp.concatenate(
+        [initial_height[None], initial_speed, jnp.concatenate(lines, axis=0)[None]], axis=0
+    )
+    gram, cross, other, full = gather_call(0, sizes, parameters, aux)
+    parameters = update_call(gram, cross, parameters, other)
+    for iteration in range(1, ITERS):
+        gram, cross, other = gather_call(iteration, sizes, parameters, full)
+        parameters = update_call(gram, cross, parameters, other)
+    return parameters
+
+
+def by_members(sizes, parameters, initial_height, initial_speed, obs_slots, *rest):
+    n_lat, n_lon, n_ens = sizes
+    blocks = n_lat * n_lon
+    members_here, rows, cols = parameters.shape[1:]
+    fits = (
+        n_ens == 2
+        and members_here % blocks == 0
+        and members_here // blocks <= rows
+        and rows == 8
+        and members_here * n_ens == blocks * 8
+        and cols == 128
+        and obs_slots.shape[2] * obs_slots.shape[3] == cols
+    )
+    arguments = (parameters, initial_height, initial_speed, obs_slots) + rest
+    if fits:
+        return per_device_members(sizes, *arguments)
+    return per_device_halo(*arguments)
+
+
 def solution(mesh):
     placed = (
         P(None, "ens", "lat", "lon"),
@@ -139,7 +550,7 @@
         P(None, ("lat", "lon"), None, None),
     )
     return jax.shard_map(
-        per_device,
+        functools.partial(by_members, tuple(mesh.shape[a] for a in ("lat", "lon", "ens"))),
         mesh=mesh,
         in_specs=placed,
         out_specs=P(None, "ens", "lat", "lon"),

time: 810 us -> 106 us (0.13); the launches traced: 800 us -> 106 us
  waiting for transfers between devices: 505 us -> 0 us
  starting transfers between devices: 173 us -> 0 us
  Pallas kernels: 0 us -> 102 us
  other arithmetic: 69.1 us -> 0.77 us
  local copies, waits for them, and re-layouts: 25.9 us -> 3.43 us
  between operations: 16.3 us -> 0.05 us
    ppermute x84 -> x0, waiting for transfers between devices: 294 us -> none  [the longest x42 150 us: padded_2(): before = lax.ppermute(last, axis, up)]
    psum x2 -> x0, waiting for transfers between devices: 210 us -> none  [per_device(): gram_part, cross_part = lax.psum((gram_part, cross_part), ('lat', 'lon'))]
    ppermute x84 -> x0, starting transfers between devices: 165 us -> none  [the longest x42 83.1 us: padded_2(): before = lax.ppermute(last, axis, up)]
    pallas_call x0 -> x4, Pallas kernels: none -> 102 us  [the longest x2 90.1 us: gather_call(): pl.pallas_call(functools.partial(gather_kernel, iteration, n_lat, n_lon,...]
    another operation x12 -> x0, other arithmetic: 45.9 us -> none  [the longest x6 24.8 us: solve_weights(): factor = jnp.linalg.cholesky(system)]
    add x26 -> x0, other arithmetic: 10.5 us -> none  [the longest x12 4.75 us: advance(): height = height - depth_step * (east_diff + north_diff) + forcing]
    slice x44 -> x0, local copies, waits for them, and re-layouts: 10.2 us -> none  [the longest x20 4.14 us: padded_2(): last = lax.slice_in_dim(value, length - width, length, axis=dim)]
    mul x11 -> x0, other arithmetic: 9.57 us -> none  [the longest x10 9.57 us: wall_rows(): return padded * keep_rows.astype(padded.dtype)]
  transfers between devices with their start and end apart: 90 -> 0, of which waited for: 57 -> 0; matrix products, arithmetic and copies ran while one was open for 8% -> 0% of each run, Pallas kernels for 0% -> 0%
where the time goes in v1:
time: 106 us
  Pallas kernels  102 us (96%)
  local copies, waits for them, and re-layouts  3.43 us (3%)
    pallas_call x2, Pallas kernels, gather_call(): pl.pallas_call(functools.partial(gather_kernel, iteration, n_lat, n_lon,...  90.1 us
    pallas_call x2, Pallas kernels, update_call(): pl.pallas_call(update_kernel, out_shape=jax.ShapeDtypeStruct(params.shape...  11.4 us
    unnamed x12, local copies, waits for them, and re-layouts  3.02 us

profile of v1, /device:TPU:0, one launch (start us, length us, event | category | flops | bytes accessed | tf_op | source)
XLA Modules:
  0.0 105.8 jit_solution(14368582980681073051)
XLA Ops:
  0.0 0.1 pad.6.clone
  0.1 0.7 convert_element_type.6
  0.8 0.1 copy.10
  0.9 0.0 copy-start.1
  0.9 0.1 convert_element_type.7
  0.9 0.6 copy-done.1
  1.6 0.1 copy.11
  1.6 0.0 copy-start.2
  1.6 0.1 reshape.8
  1.7 0.6 copy-done.2
  2.3 0.1 copy.12
  2.4 0.0 copy-start.3
  2.4 0.1 reshape.9
  2.5 0.0 copy-start.4
  2.5 0.1 maximum_bitcast_fusion
  2.6 0.5 copy-done.3
  3.1 0.1 copy-done.4
  3.2 0.0 copy-start
  3.2 1.0 copy-done
  4.2 50.1 %shard_map.64 = (f32[128,128]{1,0:T(8,128)S(1)}, f32[128,128]{1,0:T(8,128)S(1)}, f32[1,2,64,8,128]{4,3,2,1,0:T(8,128)S(1)}, f32[16,4,8,128]{3,2,1,0:T(8,128)S(1)}) custom-call(f32[2,64,8,128]{3,2,1,0:T(8,128)S(1)} %copy-done, f32[4,8,128]{2,1,0:T(8,128)S(1)} %pad_maximum_fusion.refs_1_), custom_call_target="tpu_custom_call" | custom-call | tf_op jit(solution)/shard_map/pallas_call | solution.py:418
  54.3 5.3 %shard_map.65.refs_0_.params = f32[2,64,8,128]{3,2,1,0:T(8,128)S(1)} custom-call(f32[128,128]{1,0:T(8,128)S(1)} %get-tuple-element.12.gram, f32[128,128]{1,0:T(8,128)S(1)} %get-tuple-element.13.cross, f32[2,64,8,128]{3,2,1,0:T(8,128)S(1)} %copy-done, f32[1,2,64,8,128]{4,3,2,1,0:T(8,128)S(1)} %get-tuple-element.14.other), custom_call_target="tpu_custom_call" | custom-call | tf_op jit(solution)/shard_map/pallas_call | solution.py:496
  59.6 40.0 %shard_map.66 = (f32[128,128]{1,0:T(8,128)S(1)}, f32[128,128]{1,0:T(8,128)S(1)}, f32[1,2,64,8,128]{4,3,2,1,0:T(8,128)S(1)}) custom-call(f32[2,64,8,128]{3,2,1,0:T(8,128)S(1)} %shard_map.65.refs_0_.params, f32[16,4,8,128]{3,2,1,0:T(8,128)S(1)} %get-tuple-element.15.refs_1_), custom_call_target="tpu_custom_call" | custom-call | tf_op jit(solution)/shard_map/pallas_call | solution.py:418
  99.7 6.1 %shard_map.67 = f32[2,64,8,128]{3,2,1,0:T(8,128)} custom-call(f32[128,128]{1,0:T(8,128)S(1)} %get-tuple-element.16.gram, f32[128,128]{1,0:T(8,128)S(1)} %get-tuple-element.17.cross, f32[2,64,8,128]{3,2,1,0:T(8,128)S(1)} %shard_map.65.refs_0_.params, f32[1,2,64,8,128]{4,3,2,1,0:T(8,128)S(1)} %get-tuple-element.18.other), custom_call_target="tpu_custom_call" | custom-call | tf_op jit(solution)/shard_map/pallas_call | solution.py:496
  (2 shorter events, 0.0 us)
Async XLA Ops:
  0.9 0.7 copy-start.1
  1.6 0.7 copy-start.2
  2.4 0.7 copy-start.3
  2.5 0.7 copy-start.4
  3.2 1.0 copy-start

commit v2 on v1

--- a/solution.py
+++ b/solution.py
@@ -166,17 +166,33 @@
     return height
 
 
+def flat_line(block, width):
+    depth, count = block.shape
+    lanes = lax.broadcasted_iota(jnp.int32, (count, width), 1)
+    slots = lax.broadcasted_iota(jnp.int32, (count, width), 0)
+    spread_out = jnp.dot(
+        block,
+        (lax.rem(lanes, count) == slots).astype(jnp.float32),
+        precision=lax.Precision.HIGHEST,
+        preferred_element_type=jnp.float32,
+    )
+    owners = lax.broadcasted_iota(jnp.int32, (depth, width), 0)
+    groups = lax.broadcasted_iota(jnp.int32, (depth, width), 1) // count
+    return jnp.sum(jnp.where(owners == groups, spread_out, 0.0), axis=0, keepdims=True)
+
+
 def gather_kernel(iteration, n_lat, n_lon, n_ens, *refs):
     first = iteration == 0
     blocks = n_lat * n_lon
     if first:
-        params, aux, gram, cross, other, full, got, send_a, recv_a = refs[:9]
-        refs = refs[9:]
+        params, start_height, start_speed, slots_in, values_in, precision_in = refs[:6]
+        gram, cross, other, full, got, aux, send_a, recv_a, send_h, recv_h = refs[6:16]
+        refs = refs[16:]
     else:
         params, full, gram, cross, other, got = refs[:6]
         refs = refs[6:]
-    (field, outgoing, arrived, part, pieces, summed, total) = refs[:7]
-    (send_p, recv_p, send_o, recv_o, send_y, recv_y, send_r, recv_r, send_t, recv_t) = refs[7:]
+    (outgoing, arrived, part, pieces, summed, total) = refs[:6]
+    (send_p, recv_p, send_o, recv_o, send_y, recv_y, send_r, recv_r, send_t, recv_t) = refs[6:]
     lat, lon, ens = (lax.axis_index("lat"), lax.axis_index("lon"), lax.axis_index("ens"))
     me = lat * n_lon + lon
     here = ens * blocks + me
@@ -216,41 +232,53 @@
         )
 
     each(everyone, greet)
+    if first:
+        lines = []
+        for ref in (slots_in, values_in, precision_in):
+            for t in range(ITERS):
+                lines.append(flat_line(ref[t, 0].astype(jnp.float32), cols))
+        lines.append(jnp.zeros((rows - len(lines), cols), jnp.float32))
+        aux[0] = start_height[...]
+        aux[1] = start_speed[0]
+        aux[2] = start_speed[1]
+        aux[3] = jnp.concatenate(lines, axis=0)
     pl.semaphore_wait(barrier, everyone - 1)
 
-    def param_copy(i):
+    partner = {"lat": lat, "lon": lon, "ens": 1 - ens}
+    half = pl.ds(2 * ens, 2)
+
+    def param_copy(j, i):
         to = lax.rem(me + i, blocks)
         return send(
-            params.at[:, pl.ds(to * mine, mine)], got.at[me], send_p.at[i], recv_p.at[i], peer(to)
+            params.at[:, to * mine + j], got.at[me, j], send_p.at[j, i], recv_p.at[j, i], peer(to)
         )
 
     def aux_copy(i):
         to = lax.rem(me + i, blocks)
-        return send(aux, full.at[me], send_a.at[i], recv_a.at[i], peer(to))
-
-    def start_params(i):
-        if first:
-            aux_copy(i).start()
-        param_copy(i).start()
-
-    each(blocks, start_params)
+        return send(aux.at[half], full.at[me, half], send_a.at[i], recv_a.at[i], peer(to))
+
+    def relay_copy():
+        return send(full.at[:, half], full.at[:, half], send_h.at[0], recv_h.at[0], partner)
+
+    if first:
+        each(blocks, lambda i: aux_copy(i).start())
+    for j in range(mine):
+        each(blocks, functools.partial(lambda j, i: param_copy(j, i).start(), j))
 
     def swap_copy(i):
         return send(
-            params, other.at[0], send_o.at[0], recv_o.at[0], {"lat": lat, "lon": lon, "ens": 1 - ens}
-        )
-
+            params, other.at[0], send_o.at[0], recv_o.at[0], partner
+        )
+
+    if first:
+        full[me, half] = aux[half]
+        each(blocks, lambda i: aux_copy(i).wait())
+        relay_copy().start()
     swap_copy(0).start()
-    got[me] = params[:, pl.ds(me * mine, mine)]
+    for j in range(mine):
+        got[me, j] = params[:, me * mine + j]
     if first:
-        full[me] = aux[...]
-
-    def end_params(i):
-        if first:
-            aux_copy(i).wait()
-        param_copy(i).wait()
-
-    each(blocks, end_params)
+        relay_copy().wait()
 
     def whole(pick):
         lines = []
@@ -258,39 +286,29 @@
             lines.append(jnp.concatenate([pick(a * n_lon + b) for b in range(n_lon)], axis=1))
         return jnp.concatenate(lines, axis=0)
 
+    row_ids = lax.broadcasted_iota(jnp.int32, (rows, cols), 0)
+
     def member(j, carry):
+        each(blocks, lambda i: param_copy(j, i).wait())
         height = run_member(
             whole(lambda b: full[b, 0]),
             whole(lambda b: full[b, 1]),
             whole(lambda b: full[b, 2]),
-            whole(lambda b: got[b, 0, j]),
-            whole(lambda b: got[b, 1, j]),
-        )
-        for a in range(n_lat):
-            for b in range(n_lon):
-                field[a * n_lon + b, j] = height[
-                    a * rows : (a + 1) * rows, b * cols : (b + 1) * cols
-                ]
+            whole(lambda b: got[b, j, 0]),
+            whole(lambda b: got[b, j, 1]),
+        )
+        for b in range(blocks):
+            cells = full[b, 3][iteration : iteration + 1].astype(jnp.int32)
+            cells = jnp.broadcast_to(cells, (rows, cols))
+            lanes = jnp.bitwise_and(cells, cols - 1)
+            hit = row_ids == jnp.right_shift(cells, cols.bit_length() - 1)
+            top, edge = ((b // n_lon) * rows, (b % n_lon) * cols)
+            tile = height[top : top + rows, edge : edge + cols]
+            found = jnp.where(hit, jnp.take_along_axis(tile, lanes, axis=1), 0.0)
+            outgoing[b, pl.ds(j, 1)] = jnp.sum(found, axis=0, keepdims=True)
         return carry
 
     lax.fori_loop(0, mine, member, 0)
-
-    row_ids = lax.broadcasted_iota(jnp.int32, (rows, cols), 0)
-
-    def pick_block(b, carry):
-        cells = full[b, 3][iteration : iteration + 1].astype(jnp.int32)
-        cells = jnp.broadcast_to(cells, (rows, cols))
-        lanes = jnp.bitwise_and(cells, cols - 1)
-        hit = row_ids == jnp.right_shift(cells, cols.bit_length() - 1)
-        found = jnp.zeros((rows, cols), jnp.float32)
-        for j in range(mine):
-            tile = jnp.take_along_axis(field[b, j], lanes, axis=1)
-            value = jnp.sum(jnp.where(hit, tile, 0.0), axis=0, keepdims=True)
-            found = jnp.where(row_ids == j, value, found)
-        outgoing[b] = found
-        return carry
-
-    lax.fori_loop(0, blocks, pick_block, 0)
 
     def answer_copy(i):
         to = lax.rem(here + i, everyone)
@@ -330,7 +348,7 @@
 
     each(everyone, lambda i: answer_copy(i).wait())
 
-    predicted = jnp.concatenate([arrived[s][:mine] for s in range(everyone)], axis=0)
+    predicted = jnp.concatenate([arrived[s] for s in range(everyone)], axis=0)
     members = predicted.shape[0]
     spread = predicted - jnp.sum(predicted, axis=0, keepdims=True) / members
     weighted = spread * precision
@@ -374,7 +392,7 @@
     swap_copy(0).wait()
 
 
-def gather_call(iteration, sizes, params, extra):
+def gather_call(iteration, sizes, params, *extra):
     n_lat, n_lon, n_ens = sizes
     blocks = n_lat * n_lon
     everyone = blocks * n_ens
@@ -391,21 +409,21 @@
         jax.ShapeDtypeStruct((1,) + params.shape, f32),
     ]
     scratch = [
-        VMEM((blocks, 2, mine, rows, cols), f32),
+        VMEM((blocks, mine, 2, rows, cols), f32),
     ]
     if first:
-        outs.append(jax.ShapeDtypeStruct((blocks,) + extra.shape, f32))
-        scratch += [dma((blocks,)), dma((blocks,))]
+        outs.append(jax.ShapeDtypeStruct((blocks, 4, rows, cols), f32))
+        scratch.append(VMEM((4, rows, cols), f32))
+        scratch += [dma((blocks,)), dma((blocks,)), dma((1,)), dma((1,))]
     scratch += [
-        VMEM((blocks, mine, rows, cols), f32),
-        VMEM((blocks, rows, cols), f32),
-        VMEM((everyone, rows, cols), f32),
+        VMEM((blocks, mine, cols), f32),
+        VMEM((everyone, mine, cols), f32),
         VMEM((blocks, lines, members), f32),
         VMEM((blocks, lines, members), f32),
         VMEM((lines, members), f32),
         VMEM((everyone, lines, members), f32),
-        dma((blocks,)),
-        dma((blocks,)),
+        dma((mine, blocks)),
+        dma((mine, blocks)),
         dma((1,)),
         dma((1,)),
         dma((everyone,)),
@@ -418,13 +436,13 @@
     return pl.pallas_call(
         functools.partial(gather_kernel, iteration, n_lat, n_lon, n_ens),
         out_shape=outs,
-        in_specs=[pl.BlockSpec(memory_space=VMEM)] * 2,
+        in_specs=[pl.BlockSpec(memory_space=VMEM)] * (1 + len(extra)),
         out_specs=[pl.BlockSpec(memory_space=VMEM)] * len(outs),
         scratch_shapes=scratch,
         compiler_params=pltpu.CompilerParams(
             collective_id=iteration, has_side_effects=True, vmem_limit_bytes=40 * 2**20
         ),
-    )(params, extra)
+    )(params, *extra)
 
 
 def with_rows(value, rows, start):
@@ -505,15 +523,10 @@
 def per_device_members(
     sizes, parameters, initial_height, initial_speed, obs_slots, obs_values, obs_precision
 ):
-    rows, cols = initial_height.shape
-    lines = [
-        v.reshape(ITERS, cols).astype(jnp.float32) for v in (obs_slots, obs_values, obs_precision)
-    ]
-    lines.append(jnp.zeros((rows - 3 * ITERS, cols), jnp.float32))
-    aux = jnp.concatenate(
-        [initial_height[None], initial_speed, jnp.concatenate(lines, axis=0)[None]], axis=0
-    )
-    gram, cross, other, full = gather_call(0, sizes, parameters, aux)
+    observations = (obs_slots, obs_values, obs_precision)
+    gram, cross, other, full = gather_call(
+        0, sizes, parameters, initial_height, initial_speed, *observations
+    )
     parameters = update_call(gram, cross, parameters, other)
     for iteration in range(1, ITERS):
         gram, cross, other = gather_call(iteration, sizes, parameters, full)

time: 106 us -> 94.8 us (0.89)
  Pallas kernels: 102 us -> 91.1 us
    pallas_call x2, Pallas kernels: 90.1 us -> 79.7 us  [gather_call(): pl.pallas_call(functools.partial(gather_kernel, iteration, n_lat, n_lon,...]
    unnamed x12 -> x13, local copies, waits for them, and re-layouts: 3.02 us -> 3.23 us
where the time goes in v2:
time: 94.8 us; the launch traced here: 94.4 us
  Pallas kernels  91.1 us (96%)
  local copies, waits for them, and re-layouts  3.23 us (3%)
    pallas_call x2, Pallas kernels, gather_call(): pl.pallas_call(functools.partial(gather_kernel, iteration, n_lat, n_lon,...  79.7 us
    pallas_call x2, Pallas kernels, update_call(): pl.pallas_call(update_kernel, out_shape=jax.ShapeDtypeStruct(params.shape...  11.4 us
    unnamed x13, local copies, waits for them, and re-layouts  3.23 us

profile of v2, /device:TPU:0, one launch (start us, length us, event | category | flops | bytes accessed | tf_op | source)
XLA Modules:
  0.0 94.4 jit_solution(4470369385003664975)
XLA Ops:
  0.0 0.0 copy-start.3
  0.0 0.8 copy.7.refs_3_
  0.8 0.0 copy-done.3
  0.8 0.0 copy-start.4
  0.8 0.1 copy.8.refs_4_
  0.9 0.6 copy-done.4
  1.5 0.0 copy-start.1
  1.5 0.0 copy-start.2
  1.5 0.1 copy.9.refs_5_
  1.6 0.6 copy-done.1
  2.2 0.0 copy-done.2
  2.2 0.0 copy-start
  2.2 1.0 %copy-done = f32[2,64,8,128]{3,2,1,0:T(8,128)S(1)} copy-done((f32[2,64,8,128]{3,2,1,0:T(8,128)S(1)}, f32[2,64,8,128]{3,2,1,0:T(8,128)}, u32[]{:S(2)}) %copy-start) | copy-done | bytes 524312
  3.2 43.9 %shard_map.64 = (f32[128,128]{1,0:T(8,128)S(1)}, f32[128,128]{1,0:T(8,128)S(1)}, f32[1,2,64,8,128]{4,3,2,1,0:T(8,128)S(1)}, f32[16,4,8,128]{3,2,1,0:T(8,128)S(1)}) custom-call(f32[2,64,8,128]{3,2,1,0:T(8,128)S(1)} %copy-done, f32[8,128]{1,0:T(8,128)S(1)} %copy-done.2, f32[2,8,128]{2,1,0:T(8,128)S(1)} %copy-done.1, s32[2,1,16,8]{3,2,1,0:T(8,128)S(1)} %copy.7.refs_3_, ...), custom_call_target="tpu_custom_call" | custom-call | tf_op jit(solution)/shard_map/pallas_call | solution.py:436
  47.1 5.3 %shard_map.65.refs_0_.params = f32[2,64,8,128]{3,2,1,0:T(8,128)S(1)} custom-call(f32[128,128]{1,0:T(8,128)S(1)} %get-tuple-element.12.gram, f32[128,128]{1,0:T(8,128)S(1)} %get-tuple-element.13.cross, f32[2,64,8,128]{3,2,1,0:T(8,128)S(1)} %copy-done, f32[1,2,64,8,128]{4,3,2,1,0:T(8,128)S(1)} %get-tuple-element.14.other), custom_call_target="tpu_custom_call" | custom-call | tf_op jit(solution)/shard_map/pallas_call | solution.py:514
  52.5 35.8 %shard_map.66 = (f32[128,128]{1,0:T(8,128)S(1)}, f32[128,128]{1,0:T(8,128)S(1)}, f32[1,2,64,8,128]{4,3,2,1,0:T(8,128)S(1)}) custom-call(f32[2,64,8,128]{3,2,1,0:T(8,128)S(1)} %shard_map.65.refs_0_.params, f32[16,4,8,128]{3,2,1,0:T(8,128)S(1)} %get-tuple-element.15.refs_1_), custom_call_target="tpu_custom_call" | custom-call | tf_op jit(solution)/shard_map/pallas_call | solution.py:436
  88.3 6.1 %shard_map.67 = f32[2,64,8,128]{3,2,1,0:T(8,128)} custom-call(f32[128,128]{1,0:T(8,128)S(1)} %get-tuple-element.16.gram, f32[128,128]{1,0:T(8,128)S(1)} %get-tuple-element.17.cross, f32[2,64,8,128]{3,2,1,0:T(8,128)S(1)} %shard_map.65.refs_0_.params, f32[1,2,64,8,128]{4,3,2,1,0:T(8,128)S(1)} %get-tuple-element.18.other), custom_call_target="tpu_custom_call" | custom-call | tf_op jit(solution)/shard_map/pallas_call | solution.py:514
Async XLA Ops:
  0.0 0.8 copy-start.3
  0.8 0.7 copy-start.4
  1.5 0.7 copy-start.1
  1.5 0.7 copy-start.2
  2.2 1.0 %copy-start = (f32[2,64,8,128]{3,2,1,0:T(8,128)S(1)}, f32[2,64,8,128]{3,2,1,0:T(8,128)}, u32[]{:S(2)}) copy-start(f32[2,64,8,128]{3,2,1,0:T(8,128)} %params.1) | copy-start | bytes 1572868

commit v3 on v2

--- a/solution.py
+++ b/solution.py
@@ -191,8 +191,10 @@
     else:
         params, full, gram, cross, other, got = refs[:6]
         refs = refs[6:]
-    (outgoing, arrived, part, pieces, summed, total) = refs[:6]
-    (send_p, recv_p, send_o, recv_o, send_y, recv_y, send_r, recv_r, send_t, recv_t) = refs[6:]
+    (held, load, outgoing, arrived, part, pieces, summed, total) = refs[:8]
+    loading = pltpu.make_async_copy(params, held, load.at[0])
+    loading.start()
+    (send_p, recv_p, send_o, recv_o, send_y, recv_y, send_r, recv_r, send_t, recv_t) = refs[8:]
     lat, lon, ens = (lax.axis_index("lat"), lax.axis_index("lon"), lax.axis_index("ens"))
     me = lat * n_lon + lon
     here = ens * blocks + me
@@ -243,6 +245,7 @@
         aux[2] = start_speed[1]
         aux[3] = jnp.concatenate(lines, axis=0)
     pl.semaphore_wait(barrier, everyone - 1)
+    loading.wait()
 
     partner = {"lat": lat, "lon": lon, "ens": 1 - ens}
     half = pl.ds(2 * ens, 2)
@@ -250,7 +253,7 @@
     def param_copy(j, i):
         to = lax.rem(me + i, blocks)
         return send(
-            params.at[:, to * mine + j], got.at[me, j], send_p.at[j, i], recv_p.at[j, i], peer(to)
+            held.at[:, to * mine + j], got.at[me, j], send_p.at[j, i], recv_p.at[j, i], peer(to)
         )
 
     def aux_copy(i):
@@ -267,7 +270,7 @@
 
     def swap_copy(i):
         return send(
-            params, other.at[0], send_o.at[0], recv_o.at[0], partner
+            held, other.at[0], send_o.at[0], recv_o.at[0], partner
         )
 
     if first:
@@ -276,7 +279,7 @@
         relay_copy().start()
     swap_copy(0).start()
     for j in range(mine):
-        got[me, j] = params[:, me * mine + j]
+        got[me, j] = held[:, me * mine + j]
     if first:
         relay_copy().wait()
 
@@ -416,6 +419,8 @@
         scratch.append(VMEM((4, rows, cols), f32))
         scratch += [dma((blocks,)), dma((blocks,)), dma((1,)), dma((1,))]
     scratch += [
+        VMEM(params.shape, f32),
+        dma((1,)),
         VMEM((blocks, mine, cols), f32),
         VMEM((everyone, mine, cols), f32),
         VMEM((blocks, lines, members), f32),
@@ -433,11 +438,12 @@
         dma((everyone,)),
         dma((everyone,)),
     ]
+    near, far = (pl.BlockSpec(memory_space=space) for space in (VMEM, pl.ANY))
     return pl.pallas_call(
         functools.partial(gather_kernel, iteration, n_lat, n_lon, n_ens),
         out_shape=outs,
-        in_specs=[pl.BlockSpec(memory_space=VMEM)] * (1 + len(extra)),
-        out_specs=[pl.BlockSpec(memory_space=VMEM)] * len(outs),
+        in_specs=[far] + [near] * len(extra),
+        out_specs=[near, near, far] + [near] * (len(outs) - 3),
         scratch_shapes=scratch,
         compiler_params=pltpu.CompilerParams(
             collective_id=iteration, has_side_effects=True, vmem_limit_bytes=40 * 2**20

time: 94.8 us -> 95.2 us (level)
  no operation moved by 1% of the time
where the time goes in v3:
time: 95.2 us; the launch traced here: 94.8 us
  Pallas kernels  91.6 us (96%)
  local copies, waits for them, and re-layouts  3.23 us (3%)
    pallas_call x2, Pallas kernels, gather_call(): pl.pallas_call(functools.partial(gather_kernel, iteration, n_lat, n_lon,...  80.1 us
    pallas_call x2, Pallas kernels, update_call(): pl.pallas_call(update_kernel, out_shape=jax.ShapeDtypeStruct(params.shape...  11.4 us
    unnamed x13, local copies, waits for them, and re-layouts  3.23 us

profile of v3, /device:TPU:0, one launch (start us, length us, event | category | flops | bytes accessed | tf_op | source)
XLA Modules:
  0.0 94.8 jit_solution(2152551835689211461)
XLA Ops:
  0.0 0.0 copy-start.3
  0.0 0.8 copy.7.refs_3_
  0.8 0.0 copy-done.3
  0.8 0.0 copy-start.4
  0.8 0.1 copy.8.refs_4_
  0.9 0.6 copy-done.4
  1.5 0.0 copy-start.1
  1.5 0.0 copy-start.2
  1.5 0.1 copy.9.refs_5_
  1.6 0.6 copy-done.1
  2.2 0.0 copy-done.2
  2.2 0.0 copy-start
  2.2 1.0 %copy-done = f32[2,64,8,128]{3,2,1,0:T(8,128)S(1)} copy-done((f32[2,64,8,128]{3,2,1,0:T(8,128)S(1)}, f32[2,64,8,128]{3,2,1,0:T(8,128)}, u32[]{:S(2)}) %copy-start) | copy-done | bytes 524312
  3.2 44.3 %shard_map.64 = (f32[128,128]{1,0:T(8,128)S(1)}, f32[128,128]{1,0:T(8,128)S(1)}, f32[1,2,64,8,128]{4,3,2,1,0:T(8,128)S(1)}, f32[16,4,8,128]{3,2,1,0:T(8,128)S(1)}) custom-call(f32[2,64,8,128]{3,2,1,0:T(8,128)S(1)} %copy-done, f32[8,128]{1,0:T(8,128)S(1)} %copy-done.2, f32[2,8,128]{2,1,0:T(8,128)S(1)} %copy-done.1, s32[2,1,16,8]{3,2,1,0:T(8,128)S(1)} %copy.7.refs_3_, ...), custom_call_target="tpu_custom_call" | custom-call | tf_op jit(solution)/shard_map/pallas_call | solution.py:442
  47.5 5.3 %shard_map.65.refs_0_.params = f32[2,64,8,128]{3,2,1,0:T(8,128)S(1)} custom-call(f32[128,128]{1,0:T(8,128)S(1)} %get-tuple-element.12.gram, f32[128,128]{1,0:T(8,128)S(1)} %get-tuple-element.13.cross, f32[2,64,8,128]{3,2,1,0:T(8,128)S(1)} %copy-done, f32[1,2,64,8,128]{4,3,2,1,0:T(8,128)S(1)} %get-tuple-element.14.other), custom_call_target="tpu_custom_call" | custom-call | tf_op jit(solution)/shard_map/pallas_call | solution.py:520
  52.9 35.8 %shard_map.66 = (f32[128,128]{1,0:T(8,128)S(1)}, f32[128,128]{1,0:T(8,128)S(1)}, f32[1,2,64,8,128]{4,3,2,1,0:T(8,128)S(1)}) custom-call(f32[2,64,8,128]{3,2,1,0:T(8,128)S(1)} %shard_map.65.refs_0_.params, f32[16,4,8,128]{3,2,1,0:T(8,128)S(1)} %get-tuple-element.15.refs_1_), custom_call_target="tpu_custom_call" | custom-call | tf_op jit(solution)/shard_map/pallas_call | solution.py:442
  88.7 6.1 %shard_map.67 = f32[2,64,8,128]{3,2,1,0:T(8,128)} custom-call(f32[128,128]{1,0:T(8,128)S(1)} %get-tuple-element.16.gram, f32[128,128]{1,0:T(8,128)S(1)} %get-tuple-element.17.cross, f32[2,64,8,128]{3,2,1,0:T(8,128)S(1)} %shard_map.65.refs_0_.params, f32[1,2,64,8,128]{4,3,2,1,0:T(8,128)S(1)} %get-tuple-element.18.other), custom_call_target="tpu_custom_call" | custom-call | tf_op jit(solution)/shard_map/pallas_call | solution.py:520
Async XLA Ops:
  0.0 0.8 copy-start.3
  0.8 0.7 copy-start.4
  1.5 0.7 copy-start.1
  1.5 0.7 copy-start.2
  2.2 1.0 %copy-start = (f32[2,64,8,128]{3,2,1,0:T(8,128)S(1)}, f32[2,64,8,128]{3,2,1,0:T(8,128)}, u32[]{:S(2)}) copy-start(f32[2,64,8,128]{3,2,1,0:T(8,128)} %params.1) | copy-start | bytes 1572868
